TPU v7x, 32 devices: a whole 2x2x4 slice. The times are simulated.
32 devices in a mesh: lon: 4 (over y, x), lat: 4 (over z), mem: 2 (over core).
Axes of the slice: x: 2, y: 2, z: 4, core: 2. Of those that a mesh axis runs over, the one named last changes fastest.
Arguments:
- north_vel: bfloat16 [2, 4, 75, 128, 512], P('mem', None, None, 'lat', 'lon'), may hold values from -6 to 6
- up_vel: bfloat16 [2, 4, 75, 128, 512], P('mem', None, None, 'lat', 'lon'), may hold values from -6 to 6
- dens_class: int32 [2, 4, 75, 128, 512], P('mem', None, None, 'lat', 'lon'), may hold values from 0 to 79
- thickness: int32 [75, 128, 512], P(None, 'lat', 'lon'), may hold values from 0 to 2000
- basin_id: int32 [128, 512], P('lat', 'lon'), may hold values from 0 to 3
Outputs:
- depth_mean: float32 [4, 4, 2, 75, 128], P('lon', None, None, None, 'lat')
- depth_spread: float32 [4, 4, 2, 75, 128], P('lon', None, None, None, 'lat')
- class_mean: float32 [4, 4, 2, 80, 128], P('lon', None, None, None, 'lat')
- class_spread: float32 [4, 4, 2, 80, 128], P('lon', None, None, None, 'lat')
Inputs may be any that keep to these rules, and one draw needn't show every extreme that they name: `basin_id`: 0 marks land; 1 to 3 name the basins. `thickness`: thousandths of a unit layer; 0 marks a cell below the sea floor.
All inputs are finite; a program needn't handle non-finite values.
Results may differ from a plain program's by a relative error of at most 0.0029.
Values sent between devices are 32-bit elements; how exact they have to be, the bound alone decides.
No kernel may reach another device: no remote copies, remote signals or barrier semaphores. Data moves between devices by JAX's collectives and lax.ppermute only.
A program may use at most 128 MiB of HBM per device.

v0:
```python
import math

import jax
import jax.numpy as jnp
from jax import lax
from jax.sharding import PartitionSpec as P

CLASSES = 80
BASINS = 3


north_unit = 0.02
up_unit = 0.01


def carried_in(shard, axis, combine, identity):
    devices, mine = (lax.axis_size(axis), lax.axis_index(axis))
    everything = jax.tree.map(lambda part: lax.all_gather(part, axis), shard)
    start = jax.tree.map(
        lambda part, zero: jnp.broadcast_to(jnp.asarray(zero, part.dtype), part.shape),
        shard,
        identity,
    )

    def lap(k, before):
        reached = k < mine
        new = combine(before, jax.tree.map(lambda part: part[k], everything))
        return jax.tree.map(lambda a, b: jnp.where(reached, a, b), new, before)

    return lax.fori_loop(0, devices, lap, start)


def class_sums(north_flux, rise_flux, dens_class, basin_id):
    months, levels, lat_rows, lon_cells = north_flux.shape
    block = 1
    for cand in range(16, 0, -1):
        if levels % cand == 0:
            block = cand
            break
    turns = months * (levels // block)
    weighted = jnp.stack([north_flux, rise_flux], 1).reshape(
        months, 2, levels // block, block, lat_rows, lon_cells
    )
    weighted = jnp.moveaxis(weighted, 2, 1).reshape(turns, 2, block, lat_rows, lon_cells)
    combined = jnp.where(
        basin_id[None, None] > 0, (basin_id[None, None] - 1) * CLASSES + dens_class, -1
    )
    combined = combined.reshape(turns, block, lat_rows, lon_cells)
    column_ids = jnp.arange(BASINS * CLASSES, dtype=jnp.int32)

    def one_block(packed):
        onehot = (packed[1][..., None] == column_ids).astype(jnp.bfloat16)
        return jnp.einsum("skji,kjiq->sqj", packed[0], onehot, preferred_element_type=jnp.float32)

    per_block = lax.map(one_block, (weighted, combined))
    per_block = per_block.reshape(months, levels // block, 2, BASINS, CLASSES, lat_rows)
    return jnp.swapaxes(jnp.sum(per_block, axis=1), 1, 2)


def local_tables(north_vel, up_vel, dens_class, thickness, basin_id, first_row, lat_total):
    months, levels, lat_rows, lon_cells = north_vel.shape
    row_index = first_row + jnp.arange(lat_rows, dtype=jnp.int32)
    latitude = (-78.0 + 156.0 * (row_index.astype(jnp.float32) + 0.5) / lat_total) * (
        math.pi / 180.0
    )
    zonal_width = jnp.cos(latitude)
    layer_depth = thickness.astype(jnp.float32) * 0.001
    wet_cells = (thickness > 0).astype(jnp.float32)
    north_flux = (
        north_vel.astype(jnp.float32)
        * (north_unit * zonal_width)[None, None, :, None]
        * layer_depth[None]
    ).astype(jnp.bfloat16)
    rise_flux = (
        up_vel.astype(jnp.float32) * (up_unit * zonal_width)[None, None, :, None] * wet_cells[None]
    ).astype(jnp.bfloat16)
    basin_masks = (
        basin_id[None] == jnp.arange(1, BASINS + 1, dtype=jnp.int32)[:, None, None]
    ).astype(jnp.bfloat16)
    north_depth = jnp.einsum(
        "mkji,bji->mbkj", north_flux, basin_masks, preferred_element_type=jnp.float32
    )
    rise_depth = jnp.einsum(
        "mkji,bji->mbkj", rise_flux, basin_masks, preferred_element_type=jnp.float32
    )
    depth_tab = jnp.stack([north_depth, rise_depth], 2)
    class_tab = class_sums(north_flux, rise_flux, dens_class, basin_id)
    return (class_tab, depth_tab)


def with_global(tables):
    return jnp.concatenate([jnp.sum(tables, axis=2, keepdims=True), tables], 2)


def add_pair(earlier, latter):
    return (earlier[0] + latter[0], earlier[1] + latter[1])


def body(north_vel, up_vel, dens_class, thickness, basin_id):
    row_count = north_vel.shape[3]
    first_row = lax.axis_index("lat") * row_count
    lat_total = row_count * lax.axis_size("lat")

    def one_member(packed):
        return local_tables(
            packed[0], packed[1], packed[2], thickness, basin_id, first_row, lat_total
        )

    class_tab, depth_tab = lax.map(one_member, (north_vel, up_vel, dens_class))
    class_tab, depth_tab = (
        lax.psum_scatter(class_tab, "lon", scatter_dimension=1, tiled=True),
        lax.psum_scatter(depth_tab, "lon", scatter_dimension=1, tiled=True),
    )
    class_reg = with_global(class_tab)
    depth_reg = with_global(depth_tab)
    class_block = jnp.sum(class_reg[:, :, :, 1], axis=-1)
    depth_block = jnp.sum(depth_reg[:, :, :, 1], axis=-1)
    carry_class, carry_depth = carried_in(
        (class_block, depth_block),
        "lat",
        add_pair,
        (jnp.zeros_like(class_block), jnp.zeros_like(depth_block)),
    )
    class_south = jnp.cumsum(class_reg[:, :, :, 1], axis=4) + carry_class[..., None]
    class_moc = jnp.stack(
        [jnp.cumsum(class_reg[:, :, :, 0], axis=3), jnp.cumsum(class_south, axis=3)], 3
    )
    depth_south = jnp.cumsum(depth_reg[:, :, :, 1], axis=4) + carry_depth[..., None]
    depth_moc = jnp.stack([jnp.cumsum(depth_reg[:, :, :, 0], axis=3), depth_south], 3)
    members = class_moc.shape[0] * lax.axis_size("mem")
    class_total, depth_total = lax.psum((jnp.sum(class_moc, 0), jnp.sum(depth_moc, 0)), "mem")
    class_mean = class_total / members
    depth_mean = depth_total / members
    class_dev, depth_dev = lax.psum(
        (
            jnp.sum(jnp.square(class_moc - class_mean), 0),
            jnp.sum(jnp.square(depth_moc - depth_mean), 0),
        ),
        "mem",
    )
    class_spread = jnp.sqrt(class_dev / (members - 1))
    depth_spread = jnp.sqrt(depth_dev / (members - 1))
    return (depth_mean, depth_spread, class_mean, class_spread)


def solution(mesh):
    in_specs = (
        P("mem", None, None, "lat", "lon"),
        P("mem", None, None, "lat", "lon"),
        P("mem", None, None, "lat", "lon"),
        P(None, "lat", "lon"),
        P("lat", "lon"),
    )
    out_specs = (
        P("lon", None, None, None, "lat"),
        P("lon", None, None, None, "lat"),
        P("lon", None, None, None, "lat"),
        P("lon", None, None, None, "lat"),
    )
    return jax.shard_map(body, mesh=mesh, in_specs=in_specs, out_specs=out_specs, check_vma=False)
```

profile of v0, /device:TPU:0, one launch (start us, length us, event | category | flops | bytes accessed | tf_op | source)
XLA Modules:
  0.0 399.0 jit_solution(3414294359119029780)
XLA Ops:
  9.1 3.1 fusion.7
  18.0 2.9 fusion.10
  21.2 2.1 fusion.16
  23.4 2.3 fusion.30
  30.3 5.4 %add_select_fusion.2 = s32[20,15,32,128]{3,2,1,0:T(8,128)} fusion(s32[20,15,32,128]{3,2,1,0:T(8,128)} %bitcast.116, s32[32,128]{1,0:T(8,128)S(1)} %add_multiply_fusion, pred[32,128]{1,0:T(8,128)(4,1)S(1)} %broadcast_compare_fusion), kind=kLoop, calls=%fused_computation.36 | loop fusion | flops 2457600 | bytes 9850880 | tf_op jit(solution)/shard_map/while/body/eval_jaxpr/jit(_where)/select_n | solution.py:45
  35.8 263.9 %while.35 = (s32[]{:T(128)}, f32[20,2,240,32]{2,3,1,0:T(8,128)}, s32[20,15,32,128]{3,2,1,0:T(8,128)}, bf16[20,2,15,32,128]{4,3,2,1,0:T(8,128)(2,1)}, s32[]{:T(128)}) while((s32[]{:T(128)}, f32[20,2,240,32]{2,3,1,0:T(8,128)}, s32[20,15,32,128]{3,2,1,0:T(8,128)}, bf16[20,2,15,32,128]{4,3,2,1,0:T(8,128)(2,1)}, s32[]{:T(128)}) %tuple.66), condition=%wide.region_5.6_spmd.clone, body=%wide.region_4.5_spmd.clone.sunk | while | flops 73728000 | bytes 2155077 | solution.py:55
  37.8 10.5 %fusion.53 = f32[1,2,240,32]{2,1,3,0:T(2,128)S(1)} fusion(s32[15,32,128]{2,0,1:T(8,128)S(1)} %bitcast.115, bf16[1,2,15,32,128]{4,3,2,1,0:T(8,128)(2,1)S(1)} %constant_dynamic-slice_fusion.5), kind=kOutput, calls=%fused_computation.4.clone.1 | convolution fusion | flops 73728000 | bytes 552960 | tf_op jit(solution)/shard_map/while/body/eval_jaxpr/while/body/eval_jaxpr/skji,kjiq->sqj/dot_general | solution.py:53
  51.0 10.5 %fusion.53 = f32[1,2,240,32]{2,1,3,0:T(2,128)S(1)} fusion(s32[15,32,128]{2,0,1:T(8,128)S(1)} %bitcast.115, bf16[1,2,15,32,128]{4,3,2,1,0:T(8,128)(2,1)S(1)} %constant_dynamic-slice_fusion.5), kind=kOutput, calls=%fused_computation.4.clone.1 | convolution fusion | flops 73728000 | bytes 552960 | tf_op jit(solution)/shard_map/while/body/eval_jaxpr/while/body/eval_jaxpr/skji,kjiq->sqj/dot_general | solution.py:53
  64.2 10.5 %fusion.53 = f32[1,2,240,32]{2,1,3,0:T(2,128)S(1)} fusion(s32[15,32,128]{2,0,1:T(8,128)S(1)} %bitcast.115, bf16[1,2,15,32,128]{4,3,2,1,0:T(8,128)(2,1)S(1)} %constant_dynamic-slice_fusion.5), kind=kOutput, calls=%fused_computation.4.clone.1 | convolution fusion | flops 73728000 | bytes 552960 | tf_op jit(solution)/shard_map/while/body/eval_jaxpr/while/body/eval_jaxpr/skji,kjiq->sqj/dot_general | solution.py:53
  77.4 10.5 %fusion.53 = f32[1,2,240,32]{2,1,3,0:T(2,128)S(1)} fusion(s32[15,32,128]{2,0,1:T(8,128)S(1)} %bitcast.115, bf16[1,2,15,32,128]{4,3,2,1,0:T(8,128)(2,1)S(1)} %constant_dynamic-slice_fusion.5), kind=kOutput, calls=%fused_computation.4.clone.1 | convolution fusion | flops 73728000 | bytes 552960 | tf_op jit(solution)/shard_map/while/body/eval_jaxpr/while/body/eval_jaxpr/skji,kjiq->sqj/dot_general | solution.py:53
  90.6 10.5 %fusion.53 = f32[1,2,240,32]{2,1,3,0:T(2,128)S(1)} fusion(s32[15,32,128]{2,0,1:T(8,128)S(1)} %bitcast.115, bf16[1,2,15,32,128]{4,3,2,1,0:T(8,128)(2,1)S(1)} %constant_dynamic-slice_fusion.5), kind=kOutput, calls=%fused_computation.4.clone.1 | convolution fusion | flops 73728000 | bytes 552960 | tf_op jit(solution)/shard_map/while/body/eval_jaxpr/while/body/eval_jaxpr/skji,kjiq->sqj/dot_general | solution.py:53
  103.8 10.5 %fusion.53 = f32[1,2,240,32]{2,1,3,0:T(2,128)S(1)} fusion(s32[15,32,128]{2,0,1:T(8,128)S(1)} %bitcast.115, bf16[1,2,15,32,128]{4,3,2,1,0:T(8,128)(2,1)S(1)} %constant_dynamic-slice_fusion.5), kind=kOutput, calls=%fused_computation.4.clone.1 | convolution fusion | flops 73728000 | bytes 552960 | tf_op jit(solution)/shard_map/while/body/eval_jaxpr/while/body/eval_jaxpr/skji,kjiq->sqj/dot_general | solution.py:53
  117.0 10.5 %fusion.53 = f32[1,2,240,32]{2,1,3,0:T(2,128)S(1)} fusion(s32[15,32,128]{2,0,1:T(8,128)S(1)} %bitcast.115, bf16[1,2,15,32,128]{4,3,2,1,0:T(8,128)(2,1)S(1)} %constant_dynamic-slice_fusion.5), kind=kOutput, calls=%fused_computation.4.clone.1 | convolution fusion | flops 73728000 | bytes 552960 | tf_op jit(solution)/shard_map/while/body/eval_jaxpr/while/body/eval_jaxpr/skji,kjiq->sqj/dot_general | solution.py:53
  130.2 10.5 %fusion.53 = f32[1,2,240,32]{2,1,3,0:T(2,128)S(1)} fusion(s32[15,32,128]{2,0,1:T(8,128)S(1)} %bitcast.115, bf16[1,2,15,32,128]{4,3,2,1,0:T(8,128)(2,1)S(1)} %constant_dynamic-slice_fusion.5), kind=kOutput, calls=%fused_computation.4.clone.1 | convolution fusion | flops 73728000 | bytes 552960 | tf_op jit(solution)/shard_map/while/body/eval_jaxpr/while/body/eval_jaxpr/skji,kjiq->sqj/dot_general | solution.py:53
  143.4 10.5 %fusion.53 = f32[1,2,240,32]{2,1,3,0:T(2,128)S(1)} fusion(s32[15,32,128]{2,0,1:T(8,128)S(1)} %bitcast.115, bf16[1,2,15,32,128]{4,3,2,1,0:T(8,128)(2,1)S(1)} %constant_dynamic-slice_fusion.5), kind=kOutput, calls=%fused_computation.4.clone.1 | convolution fusion | flops 73728000 | bytes 552960 | tf_op jit(solution)/shard_map/while/body/eval_jaxpr/while/body/eval_jaxpr/skji,kjiq->sqj/dot_general | solution.py:53
  156.6 10.5 %fusion.53 = f32[1,2,240,32]{2,1,3,0:T(2,128)S(1)} fusion(s32[15,32,128]{2,0,1:T(8,128)S(1)} %bitcast.115, bf16[1,2,15,32,128]{4,3,2,1,0:T(8,128)(2,1)S(1)} %constant_dynamic-slice_fusion.5), kind=kOutput, calls=%fused_computation.4.clone.1 | convolution fusion | flops 73728000 | bytes 552960 | tf_op jit(solution)/shard_map/while/body/eval_jaxpr/while/body/eval_jaxpr/skji,kjiq->sqj/dot_general | solution.py:53
  169.8 10.5 %fusion.53 = f32[1,2,240,32]{2,1,3,0:T(2,128)S(1)} fusion(s32[15,32,128]{2,0,1:T(8,128)S(1)} %bitcast.115, bf16[1,2,15,32,128]{4,3,2,1,0:T(8,128)(2,1)S(1)} %constant_dynamic-slice_fusion.5), kind=kOutput, calls=%fused_computation.4.clone.1 | convolution fusion | flops 73728000 | bytes 552960 | tf_op jit(solution)/shard_map/while/body/eval_jaxpr/while/body/eval_jaxpr/skji,kjiq->sqj/dot_general | solution.py:53
  183.0 10.5 %fusion.53 = f32[1,2,240,32]{2,1,3,0:T(2,128)S(1)} fusion(s32[15,32,128]{2,0,1:T(8,128)S(1)} %bitcast.115, bf16[1,2,15,32,128]{4,3,2,1,0:T(8,128)(2,1)S(1)} %constant_dynamic-slice_fusion.5), kind=kOutput, calls=%fused_computation.4.clone.1 | convolution fusion | flops 73728000 | bytes 552960 | tf_op jit(solution)/shard_map/while/body/eval_jaxpr/while/body/eval_jaxpr/skji,kjiq->sqj/dot_general | solution.py:53
  196.2 10.5 %fusion.53 = f32[1,2,240,32]{2,1,3,0:T(2,128)S(1)} fusion(s32[15,32,128]{2,0,1:T(8,128)S(1)} %bitcast.115, bf16[1,2,15,32,128]{4,3,2,1,0:T(8,128)(2,1)S(1)} %constant_dynamic-slice_fusion.5), kind=kOutput, calls=%fused_computation.4.clone.1 | convolution fusion | flops 73728000 | bytes 552960 | tf_op jit(solution)/shard_map/while/body/eval_jaxpr/while/body/eval_jaxpr/skji,kjiq->sqj/dot_general | solution.py:53
  209.4 10.5 %fusion.53 = f32[1,2,240,32]{2,1,3,0:T(2,128)S(1)} fusion(s32[15,32,128]{2,0,1:T(8,128)S(1)} %bitcast.115, bf16[1,2,15,32,128]{4,3,2,1,0:T(8,128)(2,1)S(1)} %constant_dynamic-slice_fusion.5), kind=kOutput, calls=%fused_computation.4.clone.1 | convolution fusion | flops 73728000 | bytes 552960 | tf_op jit(solution)/shard_map/while/body/eval_jaxpr/while/body/eval_jaxpr/skji,kjiq->sqj/dot_general | solution.py:53
  222.6 10.5 %fusion.53 = f32[1,2,240,32]{2,1,3,0:T(2,128)S(1)} fusion(s32[15,32,128]{2,0,1:T(8,128)S(1)} %bitcast.115, bf16[1,2,15,32,128]{4,3,2,1,0:T(8,128)(2,1)S(1)} %constant_dynamic-slice_fusion.5), kind=kOutput, calls=%fused_computation.4.clone.1 | convolution fusion | flops 73728000 | bytes 552960 | tf_op jit(solution)/shard_map/while/body/eval_jaxpr/while/body/eval_jaxpr/skji,kjiq->sqj/dot_general | solution.py:53
  235.8 10.5 %fusion.53 = f32[1,2,240,32]{2,1,3,0:T(2,128)S(1)} fusion(s32[15,32,128]{2,0,1:T(8,128)S(1)} %bitcast.115, bf16[1,2,15,32,128]{4,3,2,1,0:T(8,128)(2,1)S(1)} %constant_dynamic-slice_fusion.5), kind=kOutput, calls=%fused_computation.4.clone.1 | convolution fusion | flops 73728000 | bytes 552960 | tf_op jit(solution)/shard_map/while/body/eval_jaxpr/while/body/eval_jaxpr/skji,kjiq->sqj/dot_general | solution.py:53
  249.0 10.5 %fusion.53 = f32[1,2,240,32]{2,1,3,0:T(2,128)S(1)} fusion(s32[15,32,128]{2,0,1:T(8,128)S(1)} %bitcast.115, bf16[1,2,15,32,128]{4,3,2,1,0:T(8,128)(2,1)S(1)} %constant_dynamic-slice_fusion.5), kind=kOutput, calls=%fused_computation.4.clone.1 | convolution fusion | flops 73728000 | bytes 552960 | tf_op jit(solution)/shard_map/while/body/eval_jaxpr/while/body/eval_jaxpr/skji,kjiq->sqj/dot_general | solution.py:53
  262.2 10.5 %fusion.53 = f32[1,2,240,32]{2,1,3,0:T(2,128)S(1)} fusion(s32[15,32,128]{2,0,1:T(8,128)S(1)} %bitcast.115, bf16[1,2,15,32,128]{4,3,2,1,0:T(8,128)(2,1)S(1)} %constant_dynamic-slice_fusion.5), kind=kOutput, calls=%fused_computation.4.clone.1 | convolution fusion | flops 73728000 | bytes 552960 | tf_op jit(solution)/shard_map/while/body/eval_jaxpr/while/body/eval_jaxpr/skji,kjiq->sqj/dot_general | solution.py:53
  275.4 10.5 %fusion.53 = f32[1,2,240,32]{2,1,3,0:T(2,128)S(1)} fusion(s32[15,32,128]{2,0,1:T(8,128)S(1)} %bitcast.115, bf16[1,2,15,32,128]{4,3,2,1,0:T(8,128)(2,1)S(1)} %constant_dynamic-slice_fusion.5), kind=kOutput, calls=%fused_computation.4.clone.1 | convolution fusion | flops 73728000 | bytes 552960 | tf_op jit(solution)/shard_map/while/body/eval_jaxpr/while/body/eval_jaxpr/skji,kjiq->sqj/dot_general | solution.py:53
  288.6 10.5 %fusion.53 = f32[1,2,240,32]{2,1,3,0:T(2,128)S(1)} fusion(s32[15,32,128]{2,0,1:T(8,128)S(1)} %bitcast.115, bf16[1,2,15,32,128]{4,3,2,1,0:T(8,128)(2,1)S(1)} %constant_dynamic-slice_fusion.5), kind=kOutput, calls=%fused_computation.4.clone.1 | convolution fusion | flops 73728000 | bytes 552960 | tf_op jit(solution)/shard_map/while/body/eval_jaxpr/while/body/eval_jaxpr/skji,kjiq->sqj/dot_general | solution.py:53
  299.7 2.9 reshape.181
  307.6 13.5 %all-gather.3 = f32[4,4,75]{2,1,0:T(4,128)S(1)} all-gather(f32[1,4,75]{2,1,0:T(4,128)S(1)} %bitcast.129), channel_id=3, replica_groups=mesh['lon'=4,'lat'=4,'mem'=2] {'lat'}, dimensions={0}, use_global_device_ids=true | all-gather | bytes 6000 | tf_op jit(solution)/shard_map/all_gather | solution.py:18
  321.2 10.6 %reduce-scatter.9.cloned.1.call-done = f32[1,1,3,2,80,32]{4,5,3,2,0,1:T(8,128)} async-done(((f32[1,4,3,2,80,32]{4,5,3,2,0,1:T(8,128)}), f32[1,1,3,2,80,32]{4,5,3,2,0,1:T(8,128)}) %reduce-scatter.9.cloned.1.call-update) | async-done | bytes 61456
  334.5 12.0 %all-gather.2 = f32[4,4,80]{2,1,0:T(4,128)S(1)} all-gather(f32[1,4,80]{2,1,0:T(4,128)S(1)} %bitcast.130), channel_id=2, replica_groups=mesh['lon'=4,'lat'=4,'mem'=2] {'lat'}, dimensions={0}, use_global_device_ids=true | all-gather | bytes 6400 | tf_op jit(solution)/shard_map/all_gather | solution.py:18
  349.5 16.8 %all-reduce.9.cloned.1.call-done = (f32[1,4,2,75,32]{3,4,2,1,0:T(8,128)}, f32[1,4,2,80,32]{3,4,2,1,0:T(8,128)}) async-done(((f32[1,4,2,75,32]{3,4,2,1,0:T(8,128)}, f32[1,4,2,80,32]{3,4,2,1,0:T(8,128)}), (f32[1,4,2,75,32]{3,4,2,1,0:T(8,128)}, f32[1,4,2,80,32]{3,4,2,1,0:T(8,128)})) %all-reduce.9.cloned.1.call-update) | async-done | bytes 158736 | tf_op jit(solution)/shard_map/psum | solution.py:131
  369.7 19.7 %all-reduce.7.cloned.1.call-done = (f32[1,4,2,75,32]{3,4,2,1,0:T(8,128)}, f32[1,4,2,80,32]{3,4,2,1,0:T(8,128)}) async-done(((f32[1,4,2,75,32]{3,4,2,1,0:T(8,128)}, f32[1,4,2,80,32]{3,4,2,1,0:T(8,128)}), (f32[1,4,2,75,32]{3,4,2,1,0:T(8,128)}, f32[1,4,2,80,32]{3,4,2,1,0:T(8,128)})) %all-reduce.7.cloned.1.call-update) | async-done | bytes 158736 | tf_op jit(solution)/shard_map/psum | solution.py:134
  (164 shorter events, 84.1 us)
Async XLA Ops:
  7.2 297.2 %reduce-scatter.7.cloned.1.call-start = ((), (), s32[]{:S(2)}) async-start(), calls=%async_computation.2 | async-start | bytes 491520
  7.2 1.7 copy-start.6
  8.9 3.3 copy-start.3
  9.0 5.1 %copy-start.1 = (f32[75,32,128]{2,1,0:T(8,128)}, f32[75,32,128]{2,1,0:T(8,128)S(1)}, u32[]{:S(2)}) copy-start(f32[75,32,128]{2,1,0:T(8,128)S(1)} %compare_convert_fusion) | copy-start | bytes 3686404
  9.1 3.1 copy-start.7
  12.2 1.9 copy-start.4
  17.8 314.0 %reduce-scatter.9.cloned.1.call-start = ((), (), s32[]{:S(2)}) async-start(), calls=%async_computation.3 | async-start | bytes 491520
  18.0 2.9 copy-start.2
  18.0 3.2 copy-start.5
  23.4 2.3 copy-start
  304.3 62.1 %all-reduce.9.cloned.1.call-start = ((), (), s32[]{:S(2)}) async-start(), calls=%async_computation.5 | async-start | bytes 524288 | tf_op jit(solution)/shard_map/psum | solution.py:131
  349.3 40.0 %all-reduce.7.cloned.1.call-start = ((), (), s32[]{:S(2)}) async-start(), calls=%async_computation.4 | async-start | bytes 524288 | tf_op jit(solution)/shard_map/psum | solution.py:134
Sparse Core Ops, SparseCore 0:
  17.9 27.4 reduce-scatter.6
  304.4 27.3 reduce-scatter.8
  349.4 16.9 all-reduce.8
  369.8 19.4 all-reduce.6
where the time goes:
time: 401 us; the launch traced here: 399 us
  matrix products  213 us (53%)
  local copies, waits for them, and re-layouts  63.7 us (16%)
  waiting for transfers between devices  47.2 us (12%)
  other arithmetic  34.8 us (9%)
  blocking collectives  25.5 us (6%)
  between operations  14 us (3%)
    dot_general x20, matrix products, one_block(): jnp.einsum('skji,kjiq->sqj', packed[0], onehot, preferred_element_type=jn...  209 us
    dynamic_slice x60, local copies, waits for them, and re-layouts, class_sums(): per_block = lax.map(one_block, (weighted, combined))  41.5 us
    all_gather x2, blocking collectives, carried_in(): everything = jax.tree.map(lambda part: lax.all_gather(part, axis), shard)  25.5 us
    psum x1, waiting for transfers between devices, body(): lax.psum((jnp.sum(jnp.square(class_moc - class_mean), 0), jnp.sum(jnp.squ...  19.7 us
    psum x1, waiting for transfers between devices, body(): lax.psum((jnp.sum(class_moc, 0), jnp.sum(depth_moc, 0)), 'mem')  16.8 us
    dynamic_update_slice x20, local copies, waits for them, and re-layouts, class_sums(): per_block = lax.map(one_block, (weighted, combined))  12.8 us
    unnamed x6, waiting for transfers between devices  10.7 us
  transfers between devices with their start and end apart: 4, of which 3 were waited for; matrix products, arithmetic and copies ran while one was open for 72% of the time, Pallas kernels for 0%

commit v1 on v0

v1 whole, which is shorter than its diff:
```python
import math

import jax
import jax.numpy as jnp
from jax import lax
from jax.experimental import pallas as pl
from jax.experimental.pallas import tpu as pltpu
from jax.sharding import PartitionSpec as P

CLASSES = 80
BASINS = 3
LOW = 8
HIGHS = CLASSES // LOW
SUB = 8
SLOTS = 256 // SUB
GROUPS = 2

north_unit = 0.02
up_unit = 0.01

F8 = jnp.float8_e4m3fn
BF = jnp.bfloat16
F32 = jnp.float32


def tables_kernel(levels, pairs, cut, mon, n_ref, u_ref, d_ref, t_ref, b_ref, w_ref, hc_ref, oc_ref, od_ref, f_s):
    def body(*accs):
        ca, da, db = accs[0:2], accs[2:4], accs[4:6]
        row = lax.broadcasted_iota(jnp.int32, (SUB, 256), 0)
        lane = lax.broadcasted_iota(jnp.int32, (SUB, 256), 1)
        diag = row == (lane & (SUB - 1))
        digits = hc_ref[...]
        offs, cn, cu = [], [], []
        for q in range(GROUPS):
            rows = slice(q * SUB, (q + 1) * SUB)
            b = b_ref[rows, :]
            offs.append(jnp.where(b > 0, (b - 1) * HIGHS, 2 * SLOTS))
            cn.append(w_ref[rows, :] * north_unit)
            cu.append(w_ref[rows, :] * up_unit)
        for p in range(pairs):
            lhs = [[] for _ in range(GROUPS)]
            rhs = [[] for _ in range(GROUPS)]
            for e in range(2):
                k = p + e * pairs
                lanes = slice(e * 128, (e + 1) * 128)
                if k >= levels:
                    for q in range(GROUPS):
                        lhs[q].append(jnp.zeros((128, 128), BF))
                        rhs[q].append(jnp.zeros((256, 128), F8))
                        f_s[q, p * 16 : (p + 1) * 16, lanes] = jnp.zeros((16, 128), BF)
                    continue
                n16 = n_ref[0, k].astype(F32)
                u16 = u_ref[0, k].astype(F32)
                for q in range(GROUPS):
                    rows = slice(q * SUB, (q + 1) * SUB)
                    t = t_ref[k, rows, :]
                    north = n16[rows] * cn[q] * (t.astype(F32) * 0.001)
                    rise = jnp.where(t > 0, u16[rows] * cu[q], 0.0)
                    flux = jnp.concatenate([north, rise], 0).astype(BF)
                    f_s[q, p * 16 : (p + 1) * 16, lanes] = flux
                    d = d_ref[0, k, rows, :]
                    high = ((d >> 3) + offs[q]).astype(F32)
                    low = (d & (LOW - 1)).astype(F32)
                    high = jnp.concatenate([high, high], 0).astype(BF)
                    low = jnp.concatenate([low, low], 0).astype(BF)
                    lhs[q].append(
                        jnp.concatenate([jnp.where(low == BF(x), flux, BF(0)) for x in range(LOW)], 0)
                    )
                    hit = jnp.concatenate([high] * 16, 0) == digits
                    rhs[q].append(jnp.where(hit, F8(1), F8(0)))
            for q in range(GROUPS):
                pltpu.matmul_push_rhs(
                    jnp.concatenate(rhs[q], 1), staging_register=p % 2, mxu_index=q, transpose=True
                )
            for q in range(GROUPS):
                pltpu.matmul_acc_lhs(ca[q], jnp.concatenate(lhs[q], 1), load_staged_rhs=p % 2)
        for q in range(GROUPS):
            b = b_ref[q * SUB : (q + 1) * SUB, :]
            mask = jnp.concatenate(
                [jnp.where(b == i + 1, 1.0, 0.0) for i in range(BASINS)] + [jnp.zeros((SUB, 128), F32)], 0
            )
            zero = jnp.zeros((32, 128), F32)
            held = jnp.concatenate(
                [
                    jnp.concatenate([mask, zero], 1),
                    jnp.concatenate([zero, mask], 1),
                    jnp.zeros((192, 256), F32),
                ],
                0,
            )
            pltpu.matmul_push_rhs(held.astype(F8), staging_register=pairs % 2, mxu_index=q, transpose=True)
        for q in range(GROUPS):
            pltpu.matmul_acc_lhs(da[q], f_s[q, 0 : cut * 16, :], load_staged_rhs=pairs % 2)
            pltpu.matmul_acc_lhs(db[q], f_s[q, cut * 16 : pairs * 16, :])
        for q in range(GROUPS):
            x = pltpu.matmul_pop(ca[q]).reshape(LOW, 2, SUB, 256)
            x = jnp.sum(jnp.where(diag[None, None], x, 0.0), axis=2)
            oc_ref[0, q, 0] = x[:, 0]
            oc_ref[0, q, 1] = x[:, 1]
        for q in range(GROUPS):
            for a, first, last in ((da[q], 0, cut), (db[q], cut, pairs)):
                x = pltpu.matmul_pop(a)[:, :128].reshape(last - first, 2, SUB, 128)
                x = jnp.sum(jnp.where(diag[None, None, :, :128], x, 0.0), axis=2)
                od_ref[0, q, 0, first:last, :] = x[:, 0]
                od_ref[0, q, 1, first:last, :] = x[:, 1]

    def acc(q, rows):
        return pltpu.ACC(q)((rows, 256), F32)

    pl.run_scoped(
        body, acc(0, 128), acc(1, 128), acc(0, cut * 16), acc(1, cut * 16),
        acc(0, (pairs - cut) * 16), acc(1, (pairs - cut) * 16),
    )


def lon_tables(order, north_vel, up_vel, dens_class, thickness, basin_id, width):
    _, levels, lat_rows, lon_cells = north_vel.shape
    pairs = (levels + 1) // 2
    cut = 24 if pairs > 24 else pairs // 2
    tall = GROUPS * SUB
    blocks = lat_rows // SUB
    digits = jnp.broadcast_to((jnp.arange(256, dtype=jnp.int32) // SUB).astype(BF)[:, None], (256, 128))
    padded = -(-pairs // 8) * 8

    def month_block():
        return pl.BlockSpec((1, levels, tall, lon_cells), lambda m, g, mon: (mon[m], 0, g, 0))

    def kernel(*refs):
        tables_kernel(levels, pairs, cut, *refs)

    return pl.pallas_call(
        kernel,
        grid_spec=pltpu.PrefetchScalarGridSpec(
            num_scalar_prefetch=1,
            grid=(order.shape[0], lat_rows // tall),
            in_specs=[
                month_block(),
                month_block(),
                month_block(),
                pl.BlockSpec((levels, tall, lon_cells), lambda m, g, mon: (0, g, 0)),
                pl.BlockSpec((tall, lon_cells), lambda m, g, mon: (g, 0)),
                pl.BlockSpec((tall, lon_cells), lambda m, g, mon: (g, 0)),
                pl.BlockSpec((256, 128), lambda m, g, mon: (0, 0)),
            ],
            out_specs=[
                pl.BlockSpec((1, GROUPS, 2, LOW, 256), lambda m, g, mon: (m, g, 0, 0, 0)),
                pl.BlockSpec((1, GROUPS, 2, padded, 128), lambda m, g, mon: (m, g, 0, 0, 0)),
            ],
            scratch_shapes=[pltpu.VMEM((GROUPS, pairs * 16, 256), BF)],
        ),
        out_shape=[
            jax.ShapeDtypeStruct((order.shape[0], blocks, 2, LOW, 256), F32),
            jax.ShapeDtypeStruct((order.shape[0], blocks, 2, padded, 128), F32),
        ],
        name="tables",
    )(order, north_vel, up_vel, dens_class, thickness, basin_id, width, digits)


def unfold(oc, od, levels):
    blocks = oc.shape[0]
    pairs = (levels + 1) // 2
    c = oc.reshape(blocks, 2, LOW, SLOTS, SUB)[:, :, :, : BASINS * HIGHS]
    c = c.reshape(blocks, 2, LOW, BASINS, HIGHS, SUB).transpose(3, 1, 4, 2, 0, 5)
    c = c.reshape(BASINS, 2, CLASSES, blocks * SUB)
    d = od[:, :, :pairs, : 2 * 32].reshape(blocks, 2, pairs, 2, 4, SUB)[:, :, :, :, :BASINS]
    d = d.transpose(4, 1, 3, 2, 0, 5).reshape(BASINS, 2, 2 * pairs, blocks * SUB)[:, :, :levels]
    return c, d


def with_global(tables):
    return jnp.concatenate([jnp.sum(tables, axis=1, keepdims=True), tables], 1)


def body(north_vel, up_vel, dens_class, thickness, basin_id):
    local_members, months, levels, row_count, lon_cells = north_vel.shape
    lons, lats, mems = lax.axis_size("lon"), lax.axis_size("lat"), lax.axis_size("mem")
    mine = lax.axis_index("lon")
    first_row = lax.axis_index("lat") * row_count
    row_index = first_row + jnp.arange(row_count, dtype=jnp.int32)
    latitude = (-78.0 + 156.0 * (row_index.astype(F32) + 0.5) / (row_count * lats)) * (math.pi / 180.0)
    width = jnp.broadcast_to(jnp.cos(latitude)[:, None], (row_count, lon_cells))
    each = months // lons
    order = jnp.concatenate(
        [((mine + s) % lons) * each + jnp.arange(each, dtype=jnp.int32) for s in range(1, lons + 1)]
    )

    def owned(table):
        total = table[(lons - 1) * each :]
        for s in range(1, lons):
            total = total + lax.ppermute(
                table[(s - 1) * each : s * each], "lon", [(i, (i + s) % lons) for i in range(lons)]
            )
        return total

    class_tabs, depth_tabs = [], []
    for e in range(local_members):
        oc, od = lon_tables(order, north_vel[e], up_vel[e], dens_class[e], thickness, basin_id, width)
        c, d = jax.vmap(lambda a, b: unfold(a, b, levels))(owned(oc), owned(od))
        class_tabs.append(c)
        depth_tabs.append(d)
    class_tab, depth_tab = jnp.stack(class_tabs), jnp.stack(depth_tabs)

    block = (jnp.sum(class_tab[:, :, :, 1], -1), jnp.sum(depth_tab[:, :, :, 1], -1))
    carry = jax.tree.map(jnp.zeros_like, block)
    for s in range(1, lats):
        moved = lax.ppermute(block, "lat", [(i, i + s) for i in range(lats - s)])
        carry = jax.tree.map(jnp.add, carry, moved)

    class_south = jnp.cumsum(jnp.cumsum(class_tab[:, :, :, 1], axis=4) + carry[0][..., None], axis=3)
    class_moc = jnp.stack([jnp.cumsum(class_tab[:, :, :, 0], axis=3), class_south], 3)
    depth_south = jnp.cumsum(depth_tab[:, :, :, 1], axis=4) + carry[1][..., None]
    depth_moc = jnp.stack([jnp.cumsum(depth_tab[:, :, :, 0], axis=3), depth_south], 3)

    members = local_members * mems
    if local_members == 1 and mems == 2:
        both = []
        for moc in (class_moc, depth_moc):
            other = lax.ppermute(moc, "mem", [(0, 1), (1, 0)])
            a, b = with_global(moc[0]), with_global(other[0])
            mean = (a + b) / members
            both.append((mean, jnp.sqrt((jnp.square(a - mean) + jnp.square(b - mean)) / (members - 1))))
        (class_mean, class_spread), (depth_mean, depth_spread) = both
    else:
        mocs = (jax.vmap(with_global)(class_moc), jax.vmap(with_global)(depth_moc))
        total = lax.psum(jax.tree.map(lambda x: jnp.sum(x, 0), mocs), "mem")
        class_mean, depth_mean = total[0] / members, total[1] / members
        dev = lax.psum(
            (
                jnp.sum(jnp.square(mocs[0] - class_mean), 0),
                jnp.sum(jnp.square(mocs[1] - depth_mean), 0),
            ),
            "mem",
        )
        class_spread = jnp.sqrt(dev[0] / (members - 1))
        depth_spread = jnp.sqrt(dev[1] / (members - 1))
    return (depth_mean, depth_spread, class_mean, class_spread)


def solution(mesh):
    in_specs = (
        P("mem", None, None, "lat", "lon"),
        P("mem", None, None, "lat", "lon"),
        P("mem", None, None, "lat", "lon"),
        P(None, "lat", "lon"),
        P("lat", "lon"),
    )
    out_specs = (
        P("lon", None, None, None, "lat"),
        P("lon", None, None, None, "lat"),
        P("lon", None, None, None, "lat"),
        P("lon", None, None, None, "lat"),
    )
    return jax.shard_map(body, mesh=mesh, in_specs=in_specs, out_specs=out_specs, check_vma=False)
```

time: 401 us -> 62.7 us (0.16)
  matrix products: 213 us -> 0 us
  local copies, waits for them, and re-layouts: 63.7 us -> 6.82 us
  waiting for transfers between devices: 47.2 us -> 8.42 us
  other arithmetic: 34.8 us -> 5.3 us
  blocking collectives: 25.5 us -> 0 us
  starting transfers between devices: 0.34 us -> 23.5 us
  Pallas kernels: 0 us -> 17.3 us
  between operations: 14 us -> 0.97 us
    dot_general x22 -> x0, matrix products: 213 us -> none  [the longest x20 209 us: one_block(): jnp.einsum('skji,kjiq->sqj', packed[0], onehot, preferred_element_type=jn...]
    dynamic_slice x60 -> x0, local copies, waits for them, and re-layouts: 41.5 us -> none  [class_sums(): per_block = lax.map(one_block, (weighted, combined))]
    psum x2 -> x0, waiting for transfers between devices: 36.5 us -> none  [the longest x1 19.7 us: body(): lax.psum((jnp.sum(jnp.square(class_moc - class_mean), 0), jnp.sum(jnp.squ...]
    all_gather x2 -> x0, blocking collectives: 25.5 us -> none  [carried_in(): everything = jax.tree.map(lambda part: lax.all_gather(part, axis), shard)]
    ppermute x0 -> x14, starting transfers between devices: none -> 23.5 us  [the longest x6 13.8 us: body(): moved = lax.ppermute(block, 'lat', [(i, i + s) for i in range(lats - s)])]
    pallas_call x0 -> x1, Pallas kernels: none -> 17.3 us  [lon_tables(): pl.pallas_call(kernel, grid_spec=pltpu.PrefetchScalarGridSpec(num_scalar_...]
    dynamic_update_slice x20 -> x0, local copies, waits for them, and re-layouts: 12.8 us -> none  [class_sums(): per_block = lax.map(one_block, (weighted, combined))]
    unnamed x6 -> x0, waiting for transfers between devices: 10.7 us -> none
  transfers between devices with their start and end apart: 4 -> 14, of which waited for: 3 -> 7; matrix products, arithmetic and copies ran while one was open for 72% -> 6% of each run, Pallas kernels for 0% -> 0%
where the time goes in v1:
time: 62.7 us; the launch traced here: 62.4 us
  starting transfers between devices  23.5 us (37%)
  Pallas kernels  17.3 us (28%)
  waiting for transfers between devices  8.42 us (13%)
  local copies, waits for them, and re-layouts  6.82 us (11%)
  other arithmetic  5.3 us (8%)
  between operations  0.97 us (2%)
    pallas_call x1, Pallas kernels, lon_tables(): pl.pallas_call(kernel, grid_spec=pltpu.PrefetchScalarGridSpec(num_scalar_...  17.3 us
    ppermute x6, starting transfers between devices, body(): moved = lax.ppermute(block, 'lat', [(i, i + s) for i in range(lats - s)])  13.8 us
    ppermute x6, starting transfers between devices, owned(): lax.ppermute(table[(s - 1) * each:s * each], 'lon', [(i, (i + s) % lons)...  9.63 us
    ppermute x6, waiting for transfers between devices, owned(): lax.ppermute(table[(s - 1) * each:s * each], 'lon', [(i, (i + s) % lons)...  7.79 us
    transpose x1, local copies, waits for them, and re-layouts, unfold(): c.reshape(blocks, 2, LOW, BASINS, HIGHS, SUB).transpose(3, 1, 4, 2, 0, 5)  1.61 us
    sqrt x2, other arithmetic, body(): jnp.sqrt((jnp.square(a - mean) + jnp.square(b - mean)) / (members - 1))  1.53 us
  transfers between devices with their start and end apart: 14, of which 7 were waited for; matrix products, arithmetic and copies ran while one was open for 6% of the time, Pallas kernels for 0%

profile of v1, /device:TPU:0, one launch (start us, length us, event | category | flops | bytes accessed | tf_op | source)
XLA Modules:
  0.0 62.4 jit_solution(13580975000779385836)
XLA Ops:
  0.8 0.6 pad_add_fusion.refs_0_
  1.4 0.7 %broadcast_in_dim.4.refs_6_ = f32[32,128]{1,0:T(8,128)} broadcast(f32[32]{0:T(128)S(1)} %multiply_cosine_fusion), dimensions={0} | broadcast | bytes 16512 | tf_op jit(solution)/shard_map/broadcast_in_dim | solution.py:181
  2.1 0.7 %broadcast_in_dim.5.refs_7_ = bf16[256,128]{1,0:T(8,128)(2,1)} broadcast(bf16[256]{0:T(256)(128)(2,1)S(1)} %fusion), dimensions={0} | broadcast | bytes 66048 | tf_op jit(solution)/shard_map/broadcast_in_dim | solution.py:122
  2.8 17.3 %tables.1 = (f32[4,4,2,8,256]{4,3,2,1,0:T(8,128)}, f32[4,4,2,40,128]{4,3,2,1,0:T(8,128)}) custom-call(s32[4]{0:T(128)} %pad_add_fusion.refs_0_, bf16[4,75,32,128]{3,2,1,0:T(8,128)(2,1)} %bitcast.41, bf16[4,75,32,128]{3,2,1,0:T(8,128)(2,1)} %bitcast.42, s32[4,75,32,128]{3,2,1,0:T(8,128)} %bitcast.38, s32[75,32,128]{2,1,0:T(8,128)} %refs_4_.1, ...), custom_call_target="tpu_custom_call" | custom-call | tf_op jit(solution)/shard_map/tables/pallas_call | solution.py:131
  20.1 0.9 %fusion.6 = (f32[1,4,2,8,256]{4,3,2,1,0:T(8,128)S(1)}, f32[1,4,2,8,256]{4,3,2,1,0:T(8,128)S(1)}, f32[1,4,2,8,256]{4,3,2,1,0:T(8,128)S(1)}) fusion(f32[4,4,2,8,256]{4,3,2,1,0:T(8,128)} %get-tuple-element.7), kind=kLoop, calls=%fused_computation.34 | loop fusion | bytes 393216 | tf_op jit(solution)/shard_map/slice | solution.py:191
  21.0 3.0 %collective-permute-start.7 = (f32[1,4,2,8,256]{4,3,2,1,0:T(8,128)S(1)}, f32[1,4,2,8,256]{4,3,2,1,0:T(8,128)S(1)}, u32[]{:S(2)}, u32[]{:S(2)}) collective-permute-start(f32[1,4,2,8,256]{4,3,2,1,0:T(8,128)S(1)} %get-tuple-element.24), channel_id=1, source_target_pairs={{0,8},{8,16},{16,24},{24,0},{1,9},{9,17},{17,25},{25,1},{2,10},{10... | collective-permute-start | bytes 196616 | tf_op jit(solution)/shard_map/ppermute | solution.py:190
  24.1 1.0 %collective-permute-start.9 = (f32[1,4,2,8,256]{4,3,2,1,0:T(8,128)S(1)}, f32[1,4,2,8,256]{4,3,2,1,0:T(8,128)S(1)}, u32[]{:S(2)}, u32[]{:S(2)}) collective-permute-start(f32[1,4,2,8,256]{4,3,2,1,0:T(8,128)S(1)} %get-tuple-element.25), channel_id=1, source_target_pairs={{0,24},{8,0},{16,8},{24,16},{1,25},{9,1},{17,9},{25,17},{2,26},{10... | collective-permute-start | bytes 196616 | tf_op jit(solution)/shard_map/ppermute | solution.py:190
  25.1 1.9 %collective-permute-start.8 = (f32[1,4,2,8,256]{4,3,2,1,0:T(8,128)S(1)}, f32[1,4,2,8,256]{4,3,2,1,0:T(8,128)S(1)}, u32[]{:S(2)}, u32[]{:S(2)}) collective-permute-start(f32[1,4,2,8,256]{4,3,2,1,0:T(8,128)S(1)} %get-tuple-element.26), channel_id=1, source_target_pairs={{0,16},{8,24},{16,0},{24,8},{1,17},{9,25},{17,1},{25,9},{2,18},{10... | collective-permute-start | bytes 196616 | tf_op jit(solution)/shard_map/ppermute | solution.py:190
  27.4 1.4 %collective-permute-done.9 = f32[1,4,2,8,256]{4,3,2,1,0:T(8,128)S(1)} collective-permute-done((f32[1,4,2,8,256]{4,3,2,1,0:T(8,128)S(1)}, f32[1,4,2,8,256]{4,3,2,1,0:T(8,128)S(1)}, u32[]{:S(2)}, u32[]{:S(2)}) %collective-permute-start.9) | collective-permute-done | bytes 65568 | tf_op jit(solution)/shard_map/ppermute | solution.py:190
  28.8 0.6 collective-permute-done.8
  29.3 0.9 %add_add_fusion = f32[1,4,2,8,256]{4,3,2,1,0:T(8,128)S(1)} fusion(f32[1,4,2,8,256]{4,3,2,1,0:T(8,128)S(1)} %collective-permute-done.9, f32[1,4,2,8,256]{4,3,2,1,0:T(8,128)S(1)} %collective-permute-done.8, f32[1,4,2,8,256]{4,3,2,1,0:T(8,128)S(1)} %collective-permute-done.7, f32[4,4,2,8,256]{4,3,2,1,0:T(8,128)} %get-tuple-element.7), kind=kLoop, calls=%fused_computation.15 | loop fusion | flops 49152 | bytes 327680 | tf_op jit(solution)/shard_map/add | solution.py:190
  30.2 0.6 reshape.476
  30.8 0.4 copy.31
  31.2 0.4 reshape.477
  31.6 1.6 %copy.32 = f32[1,3,2,10,8,4,8]{6,5,4,3,2,1,0:T(4,128)S(1)} copy(f32[1,3,2,10,8,4,8]{3,1,6,4,2,5,0:T(4,128)S(1)} %bitcast.40) | data formatting | bytes 122880 | tf_op jit(solution)/shard_map/vmap()/transpose | solution.py:163
  33.3 0.4 reshape.478
  33.8 5.9 %collective-permute-start.12 = (f32[1,1,3,80]{3,2,1,0:T(4,128)S(1)}, f32[1,1,3,80]{3,2,1,0:T(4,128)S(1)}, u32[]{:S(2)}, u32[]{:S(2)}) collective-permute-start(f32[1,1,3,80]{3,2,1,0:T(4,128)S(1)} %bitcast.50), channel_id=1, source_target_pairs={{0,6},{1,7},{8,14},{9,15},{16,22},{17,23},{24,30},{25,31}} | collective-permute-start | bytes 2888 | tf_op jit(solution)/shard_map/ppermute | solution.py:206
  39.8 1.3 %collective-permute-start.11 = (f32[1,1,3,80]{3,2,1,0:T(4,128)S(1)}, f32[1,1,3,80]{3,2,1,0:T(4,128)S(1)}, u32[]{:S(2)}, u32[]{:S(2)}) collective-permute-start(f32[1,1,3,80]{3,2,1,0:T(4,128)S(1)} %bitcast.51), channel_id=1, source_target_pairs={{0,4},{2,6},{1,5},{3,7},{8,12},{10,14},{9,13},{11,15},{16,20},{18,... | collective-permute-start | bytes 2888 | tf_op jit(solution)/shard_map/ppermute | solution.py:206
  41.1 2.5 %collective-permute-start.10 = (f32[1,1,3,80]{3,2,1,0:T(4,128)S(1)}, f32[1,1,3,80]{3,2,1,0:T(4,128)S(1)}, u32[]{:S(2)}, u32[]{:S(2)}) collective-permute-start(f32[1,1,3,80]{3,2,1,0:T(4,128)S(1)} %bitcast.52), channel_id=1, source_target_pairs={{0,2},{2,4},{4,6},{1,3},{3,5},{5,7},{8,10},{10,12},{12,14},{9,11},... | collective-permute-start | bytes 2888 | tf_op jit(solution)/shard_map/ppermute | solution.py:206
  43.6 1.8 %collective-permute-start.2 = (f32[1,4,2,40,128]{4,3,2,1,0:T(8,128)S(1)}, f32[1,4,2,40,128]{4,3,2,1,0:T(8,128)S(1)}, u32[]{:S(2)}, u32[]{:S(2)}) collective-permute-start(f32[1,4,2,40,128]{4,3,2,1,0:T(8,128)S(1)} %get-tuple-element.21), channel_id=1, source_target_pairs={{0,24},{8,0},{16,8},{24,16},{1,25},{9,1},{17,9},{25,17},{2,26},{10... | collective-permute-start | bytes 491528 | tf_op jit(solution)/shard_map/ppermute | solution.py:190
  45.4 1.2 %collective-permute-start.1 = (f32[1,4,2,40,128]{4,3,2,1,0:T(8,128)S(1)}, f32[1,4,2,40,128]{4,3,2,1,0:T(8,128)S(1)}, u32[]{:S(2)}, u32[]{:S(2)}) collective-permute-start(f32[1,4,2,40,128]{4,3,2,1,0:T(8,128)S(1)} %get-tuple-element.22), channel_id=1, source_target_pairs={{0,16},{8,24},{16,0},{24,8},{1,17},{9,25},{17,1},{25,9},{2,18},{10... | collective-permute-start | bytes 491528 | tf_op jit(solution)/shard_map/ppermute | solution.py:190
  46.8 0.7 %reduce_window_sum.53 = f32[1,1,3,1,80,32]{5,4,3,2,1,0:T(8,128)S(1)} reduce-window(f32[1,1,3,1,80,32]{5,4,3,2,1,0:T(8,128)S(1)} %get-tuple-element.29, f32[]{:T(128)} %constant.87.clone.1), window={size=1x1x1x1x1x32 pad=0_0x0_0x0_0x0_0x0_0x31_0}, to_apply=%region_6.7 | reduce-window | flops 238080 | bytes 61444 | tf_op jit(solution)/shard_map/jit(cumsum)/reduce_window_sum | solution.py:209
  47.5 0.7 %collective-permute-start = (f32[1,4,2,40,128]{4,3,2,1,0:T(8,128)S(1)}, f32[1,4,2,40,128]{4,3,2,1,0:T(8,128)S(1)}, u32[]{:S(2)}, u32[]{:S(2)}) collective-permute-start(f32[1,4,2,40,128]{4,3,2,1,0:T(8,128)S(1)} %get-tuple-element.23), channel_id=1, source_target_pairs={{0,8},{8,16},{16,24},{24,0},{1,9},{9,17},{17,25},{25,1},{2,10},{10... | collective-permute-start | bytes 491528 | tf_op jit(solution)/shard_map/ppermute | solution.py:190
  48.6 1.2 %collective-permute-done.2 = f32[1,4,2,40,128]{4,3,2,1,0:T(8,128)S(1)} collective-permute-done((f32[1,4,2,40,128]{4,3,2,1,0:T(8,128)S(1)}, f32[1,4,2,40,128]{4,3,2,1,0:T(8,128)S(1)}, u32[]{:S(2)}, u32[]{:S(2)}) %collective-permute-start.2) | collective-permute-done | bytes 163872 | tf_op jit(solution)/shard_map/ppermute | solution.py:190
  49.8 4.2 %collective-permute-done.1 = f32[1,4,2,40,128]{4,3,2,1,0:T(8,128)S(1)} collective-permute-done((f32[1,4,2,40,128]{4,3,2,1,0:T(8,128)S(1)}, f32[1,4,2,40,128]{4,3,2,1,0:T(8,128)S(1)}, u32[]{:S(2)}, u32[]{:S(2)}) %collective-permute-start.1) | collective-permute-done | bytes 163872 | tf_op jit(solution)/shard_map/ppermute | solution.py:190
  54.6 1.3 %collective-permute-start.5 = (f32[1,1,3,75]{3,2,1,0:T(4,128)S(1)}, f32[1,1,3,75]{3,2,1,0:T(4,128)S(1)}, u32[]{:S(2)}, u32[]{:S(2)}) collective-permute-start(f32[1,1,3,75]{3,2,1,0:T(4,128)S(1)} %bitcast.53), channel_id=1, source_target_pairs={{0,6},{1,7},{8,14},{9,15},{16,22},{17,23},{24,30},{25,31}} | collective-permute-start | bytes 2708 | tf_op jit(solution)/shard_map/ppermute | solution.py:206
  55.9 1.3 %collective-permute-start.4 = (f32[1,1,3,75]{3,2,1,0:T(4,128)S(1)}, f32[1,1,3,75]{3,2,1,0:T(4,128)S(1)}, u32[]{:S(2)}, u32[]{:S(2)}) collective-permute-start(f32[1,1,3,75]{3,2,1,0:T(4,128)S(1)} %bitcast.54), channel_id=1, source_target_pairs={{0,4},{2,6},{1,5},{3,7},{8,12},{10,14},{9,13},{11,15},{16,20},{18,... | collective-permute-start | bytes 2708 | tf_op jit(solution)/shard_map/ppermute | solution.py:206
  57.2 1.5 %collective-permute-start.3 = (f32[1,1,3,75]{3,2,1,0:T(4,128)S(1)}, f32[1,1,3,75]{3,2,1,0:T(4,128)S(1)}, u32[]{:S(2)}, u32[]{:S(2)}) collective-permute-start(f32[1,1,3,75]{3,2,1,0:T(4,128)S(1)} %bitcast.55), channel_id=1, source_target_pairs={{0,2},{2,4},{4,6},{1,3},{3,5},{5,7},{8,10},{10,12},{12,14},{9,11},... | collective-permute-start | bytes 2708 | tf_op jit(solution)/shard_map/ppermute | solution.py:206
  59.2 0.6 %reduce_window_sum.51 = f32[1,1,3,1,75,32]{5,4,3,2,1,0:T(8,128)S(1)} reduce-window(f32[1,1,3,1,75,32]{5,4,3,2,1,0:T(8,128)S(1)} %copy.28, f32[]{:T(128)} %constant.87.clone.1), window={size=1x1x1x1x1x32 pad=0_0x0_0x0_0x0_0x0_0x31_0}, to_apply=%region_1.2 | reduce-window | flops 223200 | bytes 57604 | tf_op jit(solution)/shard_map/jit(cumsum)/reduce_window_sum | solution.py:211
  60.3 0.8 %add_sqrt_fusion = (f32[1,4,2,80,32]{3,4,2,1,0:T(8,128)}, f32[1,4,2,80,32]{3,4,2,1,0:T(8,128)}) fusion(f32[1,3,2,80,32]{3,4,2,1,0:T(8,128)S(1)} %bitcast.44, f32[1,1,2,80,32]{3,4,2,1,0:T(8,128)S(1)} %bitcast.48, f32[1,3,2,80,32]{3,4,2,1,0:T(8,128)S(1)} %get-tuple-element.31, f32[1,1,2,80,32]{3,4,2,1,0:T(8,128)S(1)} %bitcast.46), kind=kLoop, calls=%fused_computation.8 | loop fusion | flops 184320 | bytes 327680 | tf_op jit(solution)/shard_map/sqrt | solution.py:221
  61.1 0.5 collective-permute-done.6
  61.6 0.8 %add_sqrt_fusion.1 = (f32[1,4,2,75,32]{3,4,2,1,0:T(8,128)}, f32[1,4,2,75,32]{3,4,2,1,0:T(8,128)}) fusion(f32[1,3,2,75,32]{3,4,2,1,0:T(8,128)S(1)} %bitcast.45, f32[1,1,2,75,32]{3,4,2,1,0:T(8,128)S(1)} %bitcast.49, f32[1,3,2,75,32]{3,4,2,1,0:T(8,128)S(1)} %get-tuple-element.34, f32[1,1,2,75,32]{3,4,2,1,0:T(8,128)S(1)} %bitcast.47), kind=kLoop, calls=%fused_computation.10 | loop fusion | flops 172800 | bytes 307200 | tf_op jit(solution)/shard_map/sqrt | solution.py:221
  (41 shorter events, 2.6 us)
Async XLA Ops:
  21.0 6.3 %collective-permute-start.7 = (f32[1,4,2,8,256]{4,3,2,1,0:T(8,128)S(1)}, f32[1,4,2,8,256]{4,3,2,1,0:T(8,128)S(1)}, u32[]{:S(2)}, u32[]{:S(2)}) collective-permute-start(f32[1,4,2,8,256]{4,3,2,1,0:T(8,128)S(1)} %get-tuple-element.24), channel_id=1, source_target_pairs={{0,8},{8,16},{16,24},{24,0},{1,9},{9,17},{17,25},{25,1},{2,10},{10... | collective-permute-start | bytes 196616 | tf_op jit(solution)/shard_map/ppermute | solution.py:190
  24.1 4.7 %collective-permute-start.9 = (f32[1,4,2,8,256]{4,3,2,1,0:T(8,128)S(1)}, f32[1,4,2,8,256]{4,3,2,1,0:T(8,128)S(1)}, u32[]{:S(2)}, u32[]{:S(2)}) collective-permute-start(f32[1,4,2,8,256]{4,3,2,1,0:T(8,128)S(1)} %get-tuple-element.25), channel_id=1, source_target_pairs={{0,24},{8,0},{16,8},{24,16},{1,25},{9,1},{17,9},{25,17},{2,26},{10... | collective-permute-start | bytes 196616 | tf_op jit(solution)/shard_map/ppermute | solution.py:190
  25.1 4.3 %collective-permute-start.8 = (f32[1,4,2,8,256]{4,3,2,1,0:T(8,128)S(1)}, f32[1,4,2,8,256]{4,3,2,1,0:T(8,128)S(1)}, u32[]{:S(2)}, u32[]{:S(2)}) collective-permute-start(f32[1,4,2,8,256]{4,3,2,1,0:T(8,128)S(1)} %get-tuple-element.26), channel_id=1, source_target_pairs={{0,16},{8,24},{16,0},{24,8},{1,17},{9,25},{17,1},{25,9},{2,18},{10... | collective-permute-start | bytes 196616 | tf_op jit(solution)/shard_map/ppermute | solution.py:190
  31.2 12.3 %copy-start = (f32[4,4,2,40,128]{4,3,2,1,0:T(8,128)S(1)}, f32[4,4,2,40,128]{4,3,2,1,0:T(8,128)}, u32[]{:S(2)}) copy-start(f32[4,4,2,40,128]{4,3,2,1,0:T(8,128)} %get-tuple-element.6) | copy-start | bytes 1966084
  33.8 13.6 %collective-permute-start.12 = (f32[1,1,3,80]{3,2,1,0:T(4,128)S(1)}, f32[1,1,3,80]{3,2,1,0:T(4,128)S(1)}, u32[]{:S(2)}, u32[]{:S(2)}) collective-permute-start(f32[1,1,3,80]{3,2,1,0:T(4,128)S(1)} %bitcast.50), channel_id=1, source_target_pairs={{0,6},{1,7},{8,14},{9,15},{16,22},{17,23},{24,30},{25,31}} | collective-permute-start | bytes 2888 | tf_op jit(solution)/shard_map/ppermute | solution.py:206
  39.8 8.4 %collective-permute-start.11 = (f32[1,1,3,80]{3,2,1,0:T(4,128)S(1)}, f32[1,1,3,80]{3,2,1,0:T(4,128)S(1)}, u32[]{:S(2)}, u32[]{:S(2)}) collective-permute-start(f32[1,1,3,80]{3,2,1,0:T(4,128)S(1)} %bitcast.51), channel_id=1, source_target_pairs={{0,4},{2,6},{1,5},{3,7},{8,12},{10,14},{9,13},{11,15},{16,20},{18,... | collective-permute-start | bytes 2888 | tf_op jit(solution)/shard_map/ppermute | solution.py:206
  41.1 7.1 %collective-permute-start.10 = (f32[1,1,3,80]{3,2,1,0:T(4,128)S(1)}, f32[1,1,3,80]{3,2,1,0:T(4,128)S(1)}, u32[]{:S(2)}, u32[]{:S(2)}) collective-permute-start(f32[1,1,3,80]{3,2,1,0:T(4,128)S(1)} %bitcast.52), channel_id=1, source_target_pairs={{0,2},{2,4},{4,6},{1,3},{3,5},{5,7},{8,10},{10,12},{12,14},{9,11},... | collective-permute-start | bytes 2888 | tf_op jit(solution)/shard_map/ppermute | solution.py:206
  43.6 6.2 %collective-permute-start.2 = (f32[1,4,2,40,128]{4,3,2,1,0:T(8,128)S(1)}, f32[1,4,2,40,128]{4,3,2,1,0:T(8,128)S(1)}, u32[]{:S(2)}, u32[]{:S(2)}) collective-permute-start(f32[1,4,2,40,128]{4,3,2,1,0:T(8,128)S(1)} %get-tuple-element.21), channel_id=1, source_target_pairs={{0,24},{8,0},{16,8},{24,16},{1,25},{9,1},{17,9},{25,17},{2,26},{10... | collective-permute-start | bytes 491528 | tf_op jit(solution)/shard_map/ppermute | solution.py:190
  45.4 8.6 %collective-permute-start.1 = (f32[1,4,2,40,128]{4,3,2,1,0:T(8,128)S(1)}, f32[1,4,2,40,128]{4,3,2,1,0:T(8,128)S(1)}, u32[]{:S(2)}, u32[]{:S(2)}) collective-permute-start(f32[1,4,2,40,128]{4,3,2,1,0:T(8,128)S(1)} %get-tuple-element.22), channel_id=1, source_target_pairs={{0,16},{8,24},{16,0},{24,8},{1,17},{9,25},{17,1},{25,9},{2,18},{10... | collective-permute-start | bytes 491528 | tf_op jit(solution)/shard_map/ppermute | solution.py:190
  47.5 6.6 %collective-permute-start = (f32[1,4,2,40,128]{4,3,2,1,0:T(8,128)S(1)}, f32[1,4,2,40,128]{4,3,2,1,0:T(8,128)S(1)}, u32[]{:S(2)}, u32[]{:S(2)}) collective-permute-start(f32[1,4,2,40,128]{4,3,2,1,0:T(8,128)S(1)} %get-tuple-element.23), channel_id=1, source_target_pairs={{0,8},{8,16},{16,24},{24,0},{1,9},{9,17},{17,25},{25,1},{2,10},{10... | collective-permute-start | bytes 491528 | tf_op jit(solution)/shard_map/ppermute | solution.py:190
  48.5 10.2 %collective-permute-start.13 = (f32[1,1,3,2,80,32]{4,5,3,2,1,0:T(8,128)S(1)}, f32[1,1,3,2,80,32]{4,5,3,2,1,0:T(8,128)S(1)}, u32[]{:S(2)}, u32[]{:S(2)}) collective-permute-start(f32[1,1,3,2,80,32]{4,5,3,2,1,0:T(8,128)S(1)} %get-tuple-element.32), channel_id=1, source_target_pairs={{0,1},{1,0},{2,3},{3,2},{4,5},{5,4},{6,7},{7,6},{8,9},{9,8},{10,11... | collective-permute-start | bytes 184328 | tf_op jit(solution)/shard_map/ppermute | solution.py:218
  54.6 5.3 %collective-permute-start.5 = (f32[1,1,3,75]{3,2,1,0:T(4,128)S(1)}, f32[1,1,3,75]{3,2,1,0:T(4,128)S(1)}, u32[]{:S(2)}, u32[]{:S(2)}) collective-permute-start(f32[1,1,3,75]{3,2,1,0:T(4,128)S(1)} %bitcast.53), channel_id=1, source_target_pairs={{0,6},{1,7},{8,14},{9,15},{16,22},{17,23},{24,30},{25,31}} | collective-permute-start | bytes 2708 | tf_op jit(solution)/shard_map/ppermute | solution.py:206
  55.9 4.0 %collective-permute-start.4 = (f32[1,1,3,75]{3,2,1,0:T(4,128)S(1)}, f32[1,1,3,75]{3,2,1,0:T(4,128)S(1)}, u32[]{:S(2)}, u32[]{:S(2)}) collective-permute-start(f32[1,1,3,75]{3,2,1,0:T(4,128)S(1)} %bitcast.54), channel_id=1, source_target_pairs={{0,4},{2,6},{1,5},{3,7},{8,12},{10,14},{9,13},{11,15},{16,20},{18,... | collective-permute-start | bytes 2708 | tf_op jit(solution)/shard_map/ppermute | solution.py:206
  57.2 2.8 %collective-permute-start.3 = (f32[1,1,3,75]{3,2,1,0:T(4,128)S(1)}, f32[1,1,3,75]{3,2,1,0:T(4,128)S(1)}, u32[]{:S(2)}, u32[]{:S(2)}) collective-permute-start(f32[1,1,3,75]{3,2,1,0:T(4,128)S(1)} %bitcast.55), channel_id=1, source_target_pairs={{0,2},{2,4},{4,6},{1,3},{3,5},{5,7},{8,10},{10,12},{12,14},{9,11},... | collective-permute-start | bytes 2708 | tf_op jit(solution)/shard_map/ppermute | solution.py:206
  60.2 1.4 %collective-permute-start.6 = (f32[1,1,3,2,75,32]{4,5,3,2,1,0:T(8,128)S(1)}, f32[1,1,3,2,75,32]{4,5,3,2,1,0:T(8,128)S(1)}, u32[]{:S(2)}, u32[]{:S(2)}) collective-permute-start(f32[1,1,3,2,75,32]{4,5,3,2,1,0:T(8,128)S(1)} %get-tuple-element.35), channel_id=1, source_target_pairs={{0,1},{1,0},{2,3},{3,2},{4,5},{5,4},{6,7},{7,6},{8,9},{9,8},{10,11... | collective-permute-start | bytes 172808 | tf_op jit(solution)/shard_map/ppermute | solution.py:218

commit v2 on v0

v2 whole, which is shorter than its diff:
```python
import functools
import math

import jax
import jax.numpy as jnp
from jax import lax
from jax.experimental import pallas as pl
from jax.experimental.pallas import tpu as pltpu
from jax.sharding import PartitionSpec as P

CLASSES = 80
BASINS = 3
LOW = 8
HIGHS = CLASSES // LOW
SUB = 8
SLOTS = 256 // SUB
UNITS = 2

north_unit = 0.02
up_unit = 0.01

F8 = jnp.float8_e4m3fn
BF = jnp.bfloat16
F32 = jnp.float32


def diagonal(parts, row, lane):
    for bit in (4, 2, 1):
        high = (row & bit) != 0
        same = ((lane & bit) != 0) == high
        merged = []
        for i in range(len(parts) // 2):
            u, v = parts[i], parts[i + len(parts) // 2]
            direct = jnp.where(high, v, u)
            other = jnp.where(high, u, v)
            if bit == 4:
                other = pltpu.roll(other, 4, 0)
            else:
                other = jnp.where(high, pltpu.roll(other, bit, 0), pltpu.roll(other, SUB - bit, 0))
            merged.append(jnp.where(same, direct, other))
        parts = merged
    return parts[0]


def tables_kernel(levels, lat_total, n_ref, u_ref, d_ref, t_ref, b_ref, o_ref, f_s):
    lat_rows = b_ref.shape[0]
    pairs = (levels + 1) // 2
    half = f_s.shape[2] // 16
    first_row = lax.axis_index("lat") * lat_rows

    def body(*accs):
        ca, da = accs[:UNITS], accs[UNITS:]
        row = lax.broadcasted_iota(jnp.int32, (SUB, 256), 0)
        lane = lax.broadcasted_iota(jnp.int32, (SUB, 256), 1)
        digits = (lax.broadcasted_iota(jnp.int32, (256, 128), 0) // SUB).astype(F32).astype(BF)
        for block in range(0, lat_rows // SUB, UNITS):
            offs, cn, cu, masks = [], [], [], []
            rows = [slice((block + q) * SUB, (block + q + 1) * SUB) for q in range(UNITS)]
            for q in range(UNITS):
                b = b_ref[rows[q], :]
                offs.append(jnp.where(b > 0, (b - 1) * HIGHS, 2 * SLOTS))
                masks.append([jnp.where(b == i + 1, 1.0, 0.0) for i in range(BASINS)])
                j = first_row + (block + q) * SUB + lax.broadcasted_iota(jnp.int32, (SUB, 128), 0)
                latitude = (-78.0 + 156.0 * (j.astype(F32) + 0.5) / lat_total) * (math.pi / 180.0)
                width = jnp.cos(latitude)
                cn.append(north_unit * width)
                cu.append(up_unit * width)

            def spot(k):
                return slice(k % half * 16, (k % half + 1) * 16), slice(k // half * 128, (k // half + 1) * 128)

            for k in range(levels, 2 * half):
                for q in range(UNITS):
                    f_s[block // UNITS, q, *spot(k)] = jnp.zeros((16, 128), BF)
            for p in range(pairs):
                lhs = [[] for _ in range(UNITS)]
                rhs = [[] for _ in range(UNITS)]
                for k in (p, p + pairs):
                    if k >= levels:
                        for q in range(UNITS):
                            lhs[q].append(jnp.zeros((2 * LOW * SUB, 128), F32))
                            rhs[q].append(jnp.zeros((256, 128), F8))
                        continue
                    both = slice(block * SUB, (block + UNITS) * SUB)
                    n16 = n_ref[0, k, both, :].astype(F32)
                    u16 = u_ref[0, k, both, :].astype(F32)
                    for q in range(UNITS):
                        part = slice(q * SUB, (q + 1) * SUB)
                        t = t_ref[k, rows[q], :]
                        north = n16[part] * cn[q] * (t.astype(F32) * 0.001)
                        rise = jnp.where(t > 0, u16[part] * cu[q], 0.0)
                        f_s[block // UNITS, q, *spot(k)] = jnp.concatenate([north, rise], 0).astype(BF)
                        d = d_ref[0, k, rows[q], :]
                        high = ((d // LOW if LOW != 8 else d >> 3) + offs[q]).astype(F32)
                        high = jnp.concatenate([high, high], 0).astype(BF)
                        low = d & (LOW - 1)
                        moving = []
                        for x in range(LOW):
                            upto = low <= x
                            moving += [jnp.where(upto, north, 0.0), jnp.where(upto, rise, 0.0)]
                        lhs[q].append(jnp.concatenate(moving, 0))
                        hit = jnp.concatenate([high] * 16, 0) == digits
                        rhs[q].append(jnp.where(hit, F8(1), F8(0)))
                for q in range(UNITS):
                    pltpu.matmul_push_rhs(
                        jnp.concatenate(rhs[q], 1), staging_register=p % 2, mxu_index=q, transpose=True
                    )
                for q in range(UNITS):
                    pltpu.matmul_acc_lhs(ca[q], jnp.concatenate(lhs[q], 1), load_staged_rhs=p % 2)
            zero = jnp.zeros((SUB, 128), F32)
            for c in range(half // SUB):
                staged = (pairs + c) % 2
                for q in range(UNITS):
                    left, right = [zero] * SLOTS, [zero] * SLOTS
                    at = 2 * BASINS * c
                    left[at : at + BASINS] = masks[q]
                    right[at + BASINS : at + 2 * BASINS] = masks[q]
                    held = jnp.concatenate([jnp.concatenate(left, 0), jnp.concatenate(right, 0)], 1)
                    pltpu.matmul_push_rhs(
                        held.astype(F8), staging_register=staged, mxu_index=q, transpose=True
                    )
                for q in range(UNITS):
                    pltpu.matmul_acc_lhs(
                        da[q], f_s[block // UNITS, q, c * 128 : (c + 1) * 128, :], load_staged_rhs=staged
                    )
            for which, acc in enumerate((ca, da)):
                for q in range(UNITS):
                    x = pltpu.matmul_pop(acc[q])
                    for s in range(2):
                        parts = [x[(2 * l + s) * SUB : (2 * l + s + 1) * SUB] for l in range(SUB)]
                        o_ref[0, which, block + q, s] = diagonal(parts, row, lane)

    accs = [pltpu.ACC(q)((2 * LOW * SUB, 256), F32) for _ in range(2) for q in range(UNITS)]
    pl.run_scoped(body, *accs)


def lon_tables(first_month, count, lat_total, lons, each, north_vel, up_vel, dens_class, thickness, basin_id):
    _, levels, lat_rows, lon_cells = north_vel.shape
    half = -(-((levels + 1) // 2) // SUB) * SUB
    months = lons * each

    def month(m):
        return (lax.axis_index("lon") * each + first_month + m) % months

    def month_block():
        return pl.BlockSpec((1, levels, lat_rows, lon_cells), lambda m: (month(m), 0, 0, 0))

    blocks = lat_rows // SUB
    return pl.pallas_call(
        functools.partial(tables_kernel, levels, lat_total),
        grid=(count,),
        in_specs=[
            month_block(),
            month_block(),
            month_block(),
            pl.BlockSpec((levels, lat_rows, lon_cells), lambda m: (0, 0, 0)),
            pl.BlockSpec((lat_rows, lon_cells), lambda m: (0, 0)),
        ],
        out_specs=pl.BlockSpec((1, 2, blocks, 2, SUB, 256), lambda m: (m, 0, 0, 0, 0, 0)),
        out_shape=jax.ShapeDtypeStruct((count, 2, blocks, 2, SUB, 256), F32),
        scratch_shapes=[pltpu.VMEM((blocks // UNITS, UNITS, half * 16, 256), BF)],
        name="tables",
    )(north_vel, up_vel, dens_class, thickness, basin_id)


def summary_kernel(*refs):
    o_ref = refs[-1]
    lane = lax.broadcasted_iota(jnp.int32, (SUB, 128), 1)
    for e, ref in enumerate(refs[:-1]):
        for w in range(2):
            for h in range(2):
                x = [ref[0, w, g, 0, :, h * 128 : (h + 1) * 128] for g in range(ref.shape[2])]
                x = sum(x[1:], x[0])
                for shift in (1, 2, 4):
                    x = x + pltpu.roll(x, 128 - shift, 1)
                o_ref[0, e, w, :, h * 128 : (h + 1) * 128] = jnp.where(lane & (SUB - 1) == 0, x, 0.0)


def carry_summary(tables):
    each, _, blocks = tables[0].shape[:3]
    spec = pl.BlockSpec((1, 2, blocks, 1, SUB, 256), lambda m: (m, 0, 0, 1, 0, 0))
    return pl.pallas_call(
        summary_kernel,
        grid=(each,),
        in_specs=[spec] * len(tables),
        out_specs=pl.BlockSpec((1, len(tables), 2, SUB, 256), lambda m: (m, 0, 0, 0, 0)),
        out_shape=jax.ShapeDtypeStruct((each, len(tables), 2, SUB, 256), F32),
        name="summary",
    )(*tables)


def packed(blocks, row, lane):
    out = []
    for h in range(2):
        u = [b[:, h * 128 : (h + 1) * 128] for b in blocks]
        u = [x if g == 0 else pltpu.roll(x, SUB * g, 1) for g, x in enumerate(u)]
        for r in range(4):
            pick = ((lane >> 3) - r) & 3
            c = jnp.where(pick == 0, u[0], jnp.where(pick == 1, u[1], jnp.where(pick == 2, u[2], u[3])))
            out.append(c if r == 0 else pltpu.roll(c, 128 - SUB * r, 1))
    return out


def finish_kernel(members, levels, stream, carries, *refs):
    tables, refs = refs[:members], refs[members:]
    moved, refs = refs[:carries], refs[carries:]
    outs = refs[-4 if members == 2 else -2 :]
    row = lax.broadcasted_iota(jnp.int32, (SUB, 128), 0)
    lane = lax.broadcasted_iota(jnp.int32, (SUB, 128), 1)
    lat_rows = outs[0].shape[-1]
    kinds = len(outs) // 2
    for w in range(2):
        tiles = []
        for e in range(members):
            blocks = [tables[e][0, w, g, 0] for g in range(4)]
            if carries:
                for s in range(1, carries + 1):
                    south = moved[s - 1][0, e, w]
                    blocks[0] = blocks[0] + jnp.where(lax.axis_index("lat") >= s, south, 0.0)
            part = packed(blocks, row, lane)
            if stream == 1:
                for shift in (1, 2, 4, 8, 16):
                    keep = lane & 31 >= shift
                    part = [x + jnp.where(keep, pltpu.roll(x, shift, 1), 0.0) for x in part]
            elif w == 1:
                for shift in (1, 2, 4):
                    part = [x + jnp.where(row >= shift, pltpu.roll(x, shift, 0), 0.0) for x in part]

            def tile(slot, part=part):
                x = part[slot // 16 * 4 + slot % 4]
                t = slot % 16 // 4
                return x if t == 0 else pltpu.roll(x, 128 - 32 * t, 1)

            tiles.append(tile)
        before = [[None] * BASINS for _ in range(members)]
        count = CLASSES // SUB if w == 0 else -(-levels // SUB)
        for i in range(count):
            moc = []
            for e in range(members):
                regions = []
                for b in range(BASINS):
                    if w == 0:
                        slot = b * HIGHS + i
                    else:
                        slot = i % 5 * 2 * BASINS + i // 5 * BASINS + b
                    x = tiles[e](slot)
                    if w == 0 or stream == 0:
                        total = jnp.broadcast_to(x[SUB - 1 : SUB], x.shape)
                        old = before[e][b]
                        if old is not None:
                            x = x + old
                            total = total + old
                        before[e][b] = total
                    regions.append(x)
                moc.append([regions[0] + regions[1] + regions[2]] + regions)
            size = min(SUB, (CLASSES if w == 0 else levels) - i * SUB)
            for r in range(BASINS + 1):
                if members == 2:
                    a, b = moc[0][r], moc[1][r]
                    values = ((a + b) * 0.5, jnp.abs(a - b) * math.sqrt(0.5))
                else:
                    values = (moc[0][r],)
                for v, ref in zip(values, outs[:kinds] if w == 1 else outs[kinds:]):
                    ref[0, r, 0, i * SUB : i * SUB + size, :] = v[:size, :lat_rows]


def finish(tables, moved, earlier, levels, stream):
    members = len(tables)
    each, _, blocks = tables[0].shape[:3]
    rows = blocks * SUB
    table = pl.BlockSpec((1, 2, blocks, 1, SUB, 256), lambda m: (m, 0, 0, stream, 0, 0))
    carry = pl.BlockSpec((1, members, 2, SUB, 256), lambda m: (m, 0, 0, 0, 0))
    sizes = [levels] * members + [CLASSES] * members

    def out_block(size):
        return pl.BlockSpec((1, BASINS + 1, 1, size, rows), lambda m: (m, 0, stream, 0, 0))

    first = members + len(moved)
    return pl.pallas_call(
        functools.partial(finish_kernel, members, levels, stream, len(moved)),
        grid=(each,),
        in_specs=[table] * members
        + [carry] * len(moved)
        + [pl.BlockSpec(memory_space=pl.ANY)] * len(earlier),
        out_specs=[out_block(size) for size in sizes],
        out_shape=[jax.ShapeDtypeStruct((each, BASINS + 1, 2, size, rows), F32) for size in sizes],
        input_output_aliases={first + i: i for i in range(len(earlier))},
        name="finish_up" if stream else "finish_north",
    )(*tables, *moved, *earlier)


def body(north_vel, up_vel, dens_class, thickness, basin_id):
    local_members, months, levels, row_count, lon_cells = north_vel.shape
    lons, lats, mems = lax.axis_size("lon"), lax.axis_size("lat"), lax.axis_size("mem")
    each = months // lons
    members = local_members * mems

    tables = []
    for e in range(local_members):
        fields = (north_vel[e], up_vel[e], dens_class[e], thickness, basin_id)
        others = lon_tables(each, (lons - 1) * each, row_count * lats, lons, each, *fields)
        arrived = [
            lax.ppermute(others[(s - 1) * each : s * each], "lon", [(i, (i + s) % lons) for i in range(lons)])
            for s in range(1, lons)
        ]
        total = lon_tables(0, each, row_count * lats, lons, each, *fields)
        for part in arrived:
            total = total + part
        tables.append(total)

    def south(summary):
        return [lax.ppermute(summary, "lat", [(i, (i + s) % lats) for i in range(lats)]) for s in range(1, lats)]

    if local_members == 1 and mems == 2:
        pair = [tables[0], lax.ppermute(tables[0], "mem", [(0, 1), (1, 0)])]
        moved = south(carry_summary(pair))
        outs = finish(pair, [], [], levels, 0)
        return tuple(finish(pair, moved, outs, levels, 1))

    mocs = []
    for table in tables:
        moved = south(carry_summary([table]))
        mocs.append(finish([table], moved, finish([table], [], [], levels, 0), levels, 1))
    outs = []
    for i in range(2):
        stack = jnp.stack([moc[i] for moc in mocs])
        mean = lax.psum(jnp.sum(stack, 0), "mem") / members
        dev = lax.psum(jnp.sum(jnp.square(stack - mean), 0), "mem")
        outs += [mean, jnp.sqrt(dev / (members - 1))]
    return tuple(outs)


def solution(mesh):
    in_specs = (
        P("mem", None, None, "lat", "lon"),
        P("mem", None, None, "lat", "lon"),
        P("mem", None, None, "lat", "lon"),
        P(None, "lat", "lon"),
        P("lat", "lon"),
    )
    out_specs = (
        P("lon", None, None, None, "lat"),
        P("lon", None, None, None, "lat"),
        P("lon", None, None, None, "lat"),
        P("lon", None, None, None, "lat"),
    )
    return jax.shard_map(body, mesh=mesh, in_specs=in_specs, out_specs=out_specs, check_vma=False)
```

time: 401 us -> 51.1 us (0.13)
  matrix products: 213 us -> 0 us
  local copies, waits for them, and re-layouts: 63.7 us -> 9.41 us
  waiting for transfers between devices: 47.2 us -> 4.21 us
  other arithmetic: 34.8 us -> 0.94 us
  blocking collectives: 25.5 us -> 0 us
  Pallas kernels: 0 us -> 24.7 us
  between operations: 14 us -> 0.67 us
  starting transfers between devices: 0.34 us -> 10.7 us
    dot_general x22 -> x0, matrix products: 213 us -> none  [the longest x20 209 us: one_block(): jnp.einsum('skji,kjiq->sqj', packed[0], onehot, preferred_element_type=jn...]
    dynamic_slice x60 -> x0, local copies, waits for them, and re-layouts: 41.5 us -> none  [class_sums(): per_block = lax.map(one_block, (weighted, combined))]
    psum x2 -> x0, waiting for transfers between devices: 36.5 us -> none  [the longest x1 19.7 us: body(): lax.psum((jnp.sum(jnp.square(class_moc - class_mean), 0), jnp.sum(jnp.squ...]
    all_gather x2 -> x0, blocking collectives: 25.5 us -> none  [carried_in(): everything = jax.tree.map(lambda part: lax.all_gather(part, axis), shard)]
    pallas_call x0 -> x5, Pallas kernels: none -> 24.7 us  [the longest x2 18.5 us: lon_tables(): pl.pallas_call(functools.partial(tables_kernel, levels, lat_total), grid=...]
    dynamic_update_slice x20 -> x0, local copies, waits for them, and re-layouts: 12.8 us -> none  [class_sums(): per_block = lax.map(one_block, (weighted, combined))]
    unnamed x6 -> x0, waiting for transfers between devices: 10.7 us -> none
    ppermute x0 -> x7, starting transfers between devices: none -> 10.7 us  [the longest x3 5.98 us: body(): lax.ppermute(others[(s - 1) * each:s * each], 'lon', [(i, (i + s) % lons)...]
  transfers between devices with their start and end apart: 4 -> 7, of which waited for: 3 -> 3; matrix products, arithmetic and copies ran while one was open for 72% -> 0% of each run, Pallas kernels for 0% -> 16%
where the time goes in v2:
time: 51.1 us; the launch traced here: 50.6 us
  Pallas kernels  24.7 us (48%)
  starting transfers between devices  10.7 us (21%)
  local copies, waits for them, and re-layouts  9.41 us (18%)
  waiting for transfers between devices  4.21 us (8%)
  other arithmetic  0.94 us (2%)
  between operations  0.67 us (1%)
    pallas_call x2, Pallas kernels, lon_tables(): pl.pallas_call(functools.partial(tables_kernel, levels, lat_total), grid=...  18.5 us
    pallas_call x4, local copies, waits for them, and re-layouts, finish(): pl.pallas_call(functools.partial(finish_kernel, members, levels, stream,...  7.08 us
    ppermute x3, starting transfers between devices, body(): lax.ppermute(others[(s - 1) * each:s * each], 'lon', [(i, (i + s) % lons)...  5.98 us
    ppermute x3, starting transfers between devices, south(): lax.ppermute(summary, 'lat', [(i, (i + s) % lats) for i in range(lats)])  4.6 us
    pallas_call x2, Pallas kernels, finish(): pl.pallas_call(functools.partial(finish_kernel, members, levels, stream,...  4.46 us
    ppermute x3, waiting for transfers between devices, south(): lax.ppermute(summary, 'lat', [(i, (i + s) % lats) for i in range(lats)])  2.87 us
    pallas_call x1, Pallas kernels, carry_summary(): pl.pallas_call(summary_kernel, grid=(each,), in_specs=[spec] * len(tables...  1.7 us
    ppermute x1, waiting for transfers between devices, body(): pair = [tables[0], lax.ppermute(tables[0], 'mem', [(0, 1), (1, 0)])]  1.33 us
  transfers between devices with their start and end apart: 7, of which 3 were waited for; matrix products, arithmetic and copies ran while one was open for 0% of the time, Pallas kernels for 16%

profile of v2, /device:TPU:0, one launch (start us, length us, event | category | flops | bytes accessed | tf_op | source)
XLA Modules:
  0.0 50.6 jit_solution(3449925977694080450)
XLA Ops:
  0.6 12.6 %tables.3 = f32[3,2,4,2,8,256]{5,4,3,2,1,0:T(8,128)} custom-call(bf16[4,75,32,128]{3,2,1,0:T(8,128)(2,1)} %bitcast.5, bf16[4,75,32,128]{3,2,1,0:T(8,128)(2,1)} %bitcast.7, s32[4,75,32,128]{3,2,1,0:T(8,128)} %bitcast.3, s32[75,32,128]{2,1,0:T(8,128)} %t_ref.3, s32[32,128]{1,0:T(8,128)} %b_ref.3), custom_call_target="tpu_custom_call" | custom-call | tf_op jit(solution)/shard_map/tables/pallas_call | solution.py:149
  13.3 1.1 %fusion = (f32[1,2,4,2,8,256]{5,4,3,2,1,0:T(8,128)S(1)}, f32[1,2,4,2,8,256]{5,4,3,2,1,0:T(8,128)S(1)}, f32[1,2,4,2,8,256]{5,4,3,2,1,0:T(8,128)S(1)}) fusion(f32[3,2,4,2,8,256]{5,4,3,2,1,0:T(8,128)} %tables.3), kind=kLoop, calls=%fused_computation.1 | loop fusion | bytes 786432 | tf_op jit(solution)/shard_map/slice | solution.py:303
  14.3 3.0 %collective-permute-start = (f32[1,2,4,2,8,256]{5,4,3,2,1,0:T(8,128)S(1)}, f32[1,2,4,2,8,256]{5,4,3,2,1,0:T(8,128)S(1)}, u32[]{:S(2)}, u32[]{:S(2)}) collective-permute-start(f32[1,2,4,2,8,256]{5,4,3,2,1,0:T(8,128)S(1)} %get-tuple-element.16), channel_id=1, source_target_pairs={{0,8},{8,16},{16,24},{24,0},{1,9},{9,17},{17,25},{25,1},{2,10},{10... | collective-permute-start | bytes 393224 | tf_op jit(solution)/shard_map/ppermute | solution.py:303
  17.3 1.0 %collective-permute-start.2 = (f32[1,2,4,2,8,256]{5,4,3,2,1,0:T(8,128)S(1)}, f32[1,2,4,2,8,256]{5,4,3,2,1,0:T(8,128)S(1)}, u32[]{:S(2)}, u32[]{:S(2)}) collective-permute-start(f32[1,2,4,2,8,256]{5,4,3,2,1,0:T(8,128)S(1)} %get-tuple-element.17), channel_id=1, source_target_pairs={{0,24},{8,0},{16,8},{24,16},{1,25},{9,1},{17,9},{25,17},{2,26},{10... | collective-permute-start | bytes 393224 | tf_op jit(solution)/shard_map/ppermute | solution.py:303
  18.4 1.9 %collective-permute-start.1 = (f32[1,2,4,2,8,256]{5,4,3,2,1,0:T(8,128)S(1)}, f32[1,2,4,2,8,256]{5,4,3,2,1,0:T(8,128)S(1)}, u32[]{:S(2)}, u32[]{:S(2)}) collective-permute-start(f32[1,2,4,2,8,256]{5,4,3,2,1,0:T(8,128)S(1)} %get-tuple-element.18), channel_id=1, source_target_pairs={{0,16},{8,24},{16,0},{24,8},{1,17},{9,25},{17,1},{25,9},{2,18},{10... | collective-permute-start | bytes 393224 | tf_op jit(solution)/shard_map/ppermute | solution.py:303
  20.3 5.9 %tables.2 = f32[1,2,4,2,8,256]{5,4,3,2,1,0:T(8,128)} custom-call(bf16[4,75,32,128]{3,2,1,0:T(8,128)(2,1)} %bitcast.6, bf16[4,75,32,128]{3,2,1,0:T(8,128)(2,1)} %bitcast.8, s32[4,75,32,128]{3,2,1,0:T(8,128)} %bitcast.4, s32[75,32,128]{2,1,0:T(8,128)} %t_ref.3, s32[32,128]{1,0:T(8,128)} %b_ref.3), custom_call_target="tpu_custom_call" | custom-call | tf_op jit(solution)/shard_map/tables/pallas_call | solution.py:149
  26.2 0.0 collective-permute-done
  26.2 0.0 collective-permute-done.2
  26.2 0.0 collective-permute-done.1
  26.2 0.9 %add_add_fusion.refs_0_ = f32[1,2,4,2,8,256]{5,4,3,2,1,0:T(8,128)S(1)} fusion(f32[1,2,4,2,8,256]{5,4,3,2,1,0:T(8,128)S(1)} %collective-permute-done.2, f32[1,2,4,2,8,256]{5,4,3,2,1,0:T(8,128)S(1)} %collective-permute-done.1, f32[1,2,4,2,8,256]{5,4,3,2,1,0:T(8,128)} %tables.2, f32[1,2,4,2,8,256]{5,4,3,2,1,0:T(8,128)S(1)} %collective-permute-done), kind=kLoop, calls=%fused_computation | loop fusion | flops 98304 | bytes 655360 | tf_op jit(solution)/shard_map/add | solution.py:308
  27.2 0.0 copy-start
  27.2 0.1 collective-permute-start.3
  27.3 1.3 %collective-permute-done.3.refs_1_ = f32[1,2,4,2,8,256]{5,4,3,2,1,0:T(8,128)S(1)} collective-permute-done((f32[1,2,4,2,8,256]{5,4,3,2,1,0:T(8,128)S(1)}, f32[1,2,4,2,8,256]{5,4,3,2,1,0:T(8,128)S(1)}, u32[]{:S(2)}, u32[]{:S(2)}) %collective-permute-start.3) | collective-permute-done | bytes 131104 | tf_op jit(solution)/shard_map/ppermute | solution.py:315
  28.6 0.0 copy-done
  28.6 0.0 copy-start.1
  28.6 0.7 %copy-done.1 = f32[1,2,4,2,8,256]{5,4,3,2,1,0:T(8,128)} copy-done((f32[1,2,4,2,8,256]{5,4,3,2,1,0:T(8,128)}, f32[1,2,4,2,8,256]{5,4,3,2,1,0:T(8,128)S(1)}, u32[]{:S(2)}) %copy-start.1) | copy-done | bytes 131096
  29.3 1.7 %summary.1 = f32[1,2,2,8,256]{4,3,2,1,0:T(8,128)} custom-call(f32[1,2,4,2,8,256]{5,4,3,2,1,0:T(8,128)} %copy-done, f32[1,2,4,2,8,256]{5,4,3,2,1,0:T(8,128)} %copy-done.1), custom_call_target="tpu_custom_call" | custom-call | tf_op jit(solution)/shard_map/summary/pallas_call | solution.py:182
  31.0 3.6 %collective-permute-start.6 = (f32[1,2,2,8,256]{4,3,2,1,0:T(8,128)}, f32[1,2,2,8,256]{4,3,2,1,0:T(8,128)S(1)}, u32[]{:S(2)}, u32[]{:S(2)}) collective-permute-start(f32[1,2,2,8,256]{4,3,2,1,0:T(8,128)} %summary.1), channel_id=1, source_target_pairs={{0,6},{2,0},{4,2},{6,4},{1,7},{3,1},{5,3},{7,5},{8,14},{10,8},{12,... | collective-permute-start | bytes 98312 | tf_op jit(solution)/shard_map/ppermute | solution.py:312
  34.6 0.0 collective-permute-start.5
  34.6 1.0 %collective-permute-start.4 = (f32[1,2,2,8,256]{4,3,2,1,0:T(8,128)}, f32[1,2,2,8,256]{4,3,2,1,0:T(8,128)S(1)}, u32[]{:S(2)}, u32[]{:S(2)}) collective-permute-start(f32[1,2,2,8,256]{4,3,2,1,0:T(8,128)} %summary.1), channel_id=1, source_target_pairs={{0,2},{2,4},{4,6},{6,0},{1,3},{3,5},{5,7},{7,1},{8,10},{10,12},{12... | collective-permute-start | bytes 98312 | tf_op jit(solution)/shard_map/ppermute | solution.py:312
  35.6 2.0 %finish_north.1 = (f32[1,4,2,75,32]{4,3,2,1,0:T(8,128)}, f32[1,4,2,75,32]{4,3,2,1,0:T(8,128)}, f32[1,4,2,80,32]{4,3,2,1,0:T(8,128)}, f32[1,4,2,80,32]{4,3,2,1,0:T(8,128)}) custom-call(f32[1,2,4,2,8,256]{5,4,3,2,1,0:T(8,128)} %copy-done, f32[1,2,4,2,8,256]{5,4,3,2,1,0:T(8,128)} %copy-done.1), custom_call_target="tpu_custom_call" | custom-call | tf_op jit(solution)/shard_map/finish_north/pallas_call | solution.py:279
  37.6 0.0 collective-permute-done.6.refs_4_
  37.6 2.1 %collective-permute-done.5.refs_3_ = f32[1,2,2,8,256]{4,3,2,1,0:T(8,128)S(1)} collective-permute-done((f32[1,2,2,8,256]{4,3,2,1,0:T(8,128)}, f32[1,2,2,8,256]{4,3,2,1,0:T(8,128)S(1)}, u32[]{:S(2)}, u32[]{:S(2)}) %collective-permute-start.5) | collective-permute-done | bytes 32800 | tf_op jit(solution)/shard_map/ppermute | solution.py:312
  39.7 0.7 %collective-permute-done.4.refs_2_ = f32[1,2,2,8,256]{4,3,2,1,0:T(8,128)S(1)} collective-permute-done((f32[1,2,2,8,256]{4,3,2,1,0:T(8,128)}, f32[1,2,2,8,256]{4,3,2,1,0:T(8,128)S(1)}, u32[]{:S(2)}, u32[]{:S(2)}) %collective-permute-start.4) | collective-permute-done | bytes 32800 | tf_op jit(solution)/shard_map/ppermute | solution.py:312
  40.5 0.0 copy-done.2
  40.5 0.0 copy-done.3
  40.5 0.6 %copy-done.4 = f32[1,2,2,8,256]{4,3,2,1,0:T(8,128)} copy-done((f32[1,2,2,8,256]{4,3,2,1,0:T(8,128)}, f32[1,2,2,8,256]{4,3,2,1,0:T(8,128)S(1)}, u32[]{:S(2)}) %copy-start.4) | copy-done | bytes 32792
  41.1 2.4 %finish_up.1 = (f32[1,4,2,75,32]{4,3,2,1,0:T(8,128)}, f32[1,4,2,75,32]{4,3,2,1,0:T(8,128)}, f32[1,4,2,80,32]{4,3,2,1,0:T(8,128)}, f32[1,4,2,80,32]{4,3,2,1,0:T(8,128)}) custom-call(f32[1,2,4,2,8,256]{5,4,3,2,1,0:T(8,128)} %copy-done, f32[1,2,4,2,8,256]{5,4,3,2,1,0:T(8,128)} %copy-done.1, ...), custom_call_target="tpu_custom_call", output_to_operand_aliasing={{0}: (5, {}), {1}: (6, {}), {2}: (7, {}), {3}: (8, {})} | custom-call | tf_op jit(solution)/shard_map/finish_up/pallas_call | solution.py:279
  43.5 1.8 %copy.13 = f32[1,4,2,75,32]{3,4,2,1,0:T(8,128)} copy(f32[1,4,2,75,32]{4,3,2,1,0:T(8,128)} %get-tuple-element.12) | data formatting | bytes 153600 | tf_op jit(solution)/shard_map/finish_up/pallas_call | solution.py:279
  45.3 1.8 %copy.14 = f32[1,4,2,75,32]{3,4,2,1,0:T(8,128)} copy(f32[1,4,2,75,32]{4,3,2,1,0:T(8,128)} %get-tuple-element.13) | data formatting | bytes 153600 | tf_op jit(solution)/shard_map/finish_up/pallas_call | solution.py:279
  47.1 1.8 %copy.15 = f32[1,4,2,80,32]{3,4,2,1,0:T(8,128)} copy(f32[1,4,2,80,32]{4,3,2,1,0:T(8,128)} %get-tuple-element.14) | data formatting | bytes 163840 | tf_op jit(solution)/shard_map/finish_up/pallas_call | solution.py:279
  48.8 1.8 %copy.16 = f32[1,4,2,80,32]{3,4,2,1,0:T(8,128)} copy(f32[1,4,2,80,32]{4,3,2,1,0:T(8,128)} %get-tuple-element.15) | data formatting | bytes 163840 | tf_op jit(solution)/shard_map/finish_up/pallas_call | solution.py:279
  (3 shorter events, 0.0 us)
Async XLA Ops:
  14.3 11.9 %collective-permute-start = (f32[1,2,4,2,8,256]{5,4,3,2,1,0:T(8,128)S(1)}, f32[1,2,4,2,8,256]{5,4,3,2,1,0:T(8,128)S(1)}, u32[]{:S(2)}, u32[]{:S(2)}) collective-permute-start(f32[1,2,4,2,8,256]{5,4,3,2,1,0:T(8,128)S(1)} %get-tuple-element.16), channel_id=1, source_target_pairs={{0,8},{8,16},{16,24},{24,0},{1,9},{9,17},{17,25},{25,1},{2,10},{10... | collective-permute-start | bytes 393224 | tf_op jit(solution)/shard_map/ppermute | solution.py:303
  17.3 8.9 %collective-permute-start.2 = (f32[1,2,4,2,8,256]{5,4,3,2,1,0:T(8,128)S(1)}, f32[1,2,4,2,8,256]{5,4,3,2,1,0:T(8,128)S(1)}, u32[]{:S(2)}, u32[]{:S(2)}) collective-permute-start(f32[1,2,4,2,8,256]{5,4,3,2,1,0:T(8,128)S(1)} %get-tuple-element.17), channel_id=1, source_target_pairs={{0,24},{8,0},{16,8},{24,16},{1,25},{9,1},{17,9},{25,17},{2,26},{10... | collective-permute-start | bytes 393224 | tf_op jit(solution)/shard_map/ppermute | solution.py:303
  18.4 7.9 %collective-permute-start.1 = (f32[1,2,4,2,8,256]{5,4,3,2,1,0:T(8,128)S(1)}, f32[1,2,4,2,8,256]{5,4,3,2,1,0:T(8,128)S(1)}, u32[]{:S(2)}, u32[]{:S(2)}) collective-permute-start(f32[1,2,4,2,8,256]{5,4,3,2,1,0:T(8,128)S(1)} %get-tuple-element.18), channel_id=1, source_target_pairs={{0,16},{8,24},{16,0},{24,8},{1,17},{9,25},{17,1},{25,9},{2,18},{10... | collective-permute-start | bytes 393224 | tf_op jit(solution)/shard_map/ppermute | solution.py:303
  27.2 1.4 %copy-start = (f32[1,2,4,2,8,256]{5,4,3,2,1,0:T(8,128)}, f32[1,2,4,2,8,256]{5,4,3,2,1,0:T(8,128)S(1)}, u32[]{:S(2)}) copy-start(f32[1,2,4,2,8,256]{5,4,3,2,1,0:T(8,128)S(1)} %add_add_fusion.refs_0_) | copy-start | bytes 393220
  27.2 1.4 %collective-permute-start.3 = (f32[1,2,4,2,8,256]{5,4,3,2,1,0:T(8,128)S(1)}, f32[1,2,4,2,8,256]{5,4,3,2,1,0:T(8,128)S(1)}, u32[]{:S(2)}, u32[]{:S(2)}) collective-permute-start(f32[1,2,4,2,8,256]{5,4,3,2,1,0:T(8,128)S(1)} %add_add_fusion.refs_0_), channel_id=1, source_target_pairs={{0,1},{1,0},{2,3},{3,2},{4,5},{5,4},{6,7},{7,6},{8,9},{9,8},{10,11... | collective-permute-start | bytes 393224 | tf_op jit(solution)/shard_map/ppermute | solution.py:315
  28.6 0.7 %copy-start.1 = (f32[1,2,4,2,8,256]{5,4,3,2,1,0:T(8,128)}, f32[1,2,4,2,8,256]{5,4,3,2,1,0:T(8,128)S(1)}, u32[]{:S(2)}) copy-start(f32[1,2,4,2,8,256]{5,4,3,2,1,0:T(8,128)S(1)} %collective-permute-done.3.refs_1_) | copy-start | bytes 393220
  31.0 6.7 %collective-permute-start.6 = (f32[1,2,2,8,256]{4,3,2,1,0:T(8,128)}, f32[1,2,2,8,256]{4,3,2,1,0:T(8,128)S(1)}, u32[]{:S(2)}, u32[]{:S(2)}) collective-permute-start(f32[1,2,2,8,256]{4,3,2,1,0:T(8,128)} %summary.1), channel_id=1, source_target_pairs={{0,6},{2,0},{4,2},{6,4},{1,7},{3,1},{5,3},{7,5},{8,14},{10,8},{12,... | collective-permute-start | bytes 98312 | tf_op jit(solution)/shard_map/ppermute | solution.py:312
  34.6 5.2 %collective-permute-start.5 = (f32[1,2,2,8,256]{4,3,2,1,0:T(8,128)}, f32[1,2,2,8,256]{4,3,2,1,0:T(8,128)S(1)}, u32[]{:S(2)}, u32[]{:S(2)}) collective-permute-start(f32[1,2,2,8,256]{4,3,2,1,0:T(8,128)} %summary.1), channel_id=1, source_target_pairs={{0,4},{2,6},{4,0},{6,2},{1,5},{3,7},{5,1},{7,3},{8,12},{10,14},{12... | collective-permute-start | bytes 98312 | tf_op jit(solution)/shard_map/ppermute | solution.py:312
  34.6 5.9 %collective-permute-start.4 = (f32[1,2,2,8,256]{4,3,2,1,0:T(8,128)}, f32[1,2,2,8,256]{4,3,2,1,0:T(8,128)S(1)}, u32[]{:S(2)}, u32[]{:S(2)}) collective-permute-start(f32[1,2,2,8,256]{4,3,2,1,0:T(8,128)} %summary.1), channel_id=1, source_target_pairs={{0,2},{2,4},{4,6},{6,0},{1,3},{3,5},{5,7},{7,1},{8,10},{10,12},{12... | collective-permute-start | bytes 98312 | tf_op jit(solution)/shard_map/ppermute | solution.py:312
  37.6 2.9 %copy-start.2 = (f32[1,2,2,8,256]{4,3,2,1,0:T(8,128)}, f32[1,2,2,8,256]{4,3,2,1,0:T(8,128)S(1)}, u32[]{:S(2)}) copy-start(f32[1,2,2,8,256]{4,3,2,1,0:T(8,128)S(1)} %collective-permute-done.6.refs_4_) | copy-start | bytes 98308
  39.7 0.8 %copy-start.3 = (f32[1,2,2,8,256]{4,3,2,1,0:T(8,128)}, f32[1,2,2,8,256]{4,3,2,1,0:T(8,128)S(1)}, u32[]{:S(2)}) copy-start(f32[1,2,2,8,256]{4,3,2,1,0:T(8,128)S(1)} %collective-permute-done.5.refs_3_) | copy-start | bytes 98308
  40.5 0.6 %copy-start.4 = (f32[1,2,2,8,256]{4,3,2,1,0:T(8,128)}, f32[1,2,2,8,256]{4,3,2,1,0:T(8,128)S(1)}, u32[]{:S(2)}) copy-start(f32[1,2,2,8,256]{4,3,2,1,0:T(8,128)S(1)} %collective-permute-done.4.refs_2_) | copy-start | bytes 98308

commit v3 on v2

v3 whole, which is shorter than its diff:
```python
import functools
import math

import jax
import jax.numpy as jnp
from jax import lax
from jax.experimental import pallas as pl
from jax.experimental.pallas import tpu as pltpu
from jax.sharding import PartitionSpec as P

CLASSES = 80
BASINS = 3
LOW = 8
HIGHS = CLASSES // LOW
SUB = 8
SLOTS = 256 // SUB
UNITS = 2

TABLES_VMEM = 60 << 20
SMALL_VMEM = 8 << 20

north_unit = 0.02
up_unit = 0.01

F8 = jnp.float8_e4m3fn
BF = jnp.bfloat16
F32 = jnp.float32


def diagonal(parts, row, lane):
    for bit in (4, 2, 1):
        high = (lane & bit) != 0
        same = ((row & bit) != 0) == high
        merged = []
        for i in range(len(parts) // 2):
            u, v = parts[i], parts[i + len(parts) // 2]
            direct = jnp.where(high, v, u)
            other = jnp.where(high, u, v)
            other = jnp.where(high, pltpu.roll(other, bit, 1), pltpu.roll(other, 128 - bit, 1))
            merged.append(jnp.where(same, direct, other))
        parts = merged
    return parts[0]


def tables_kernel(levels, lat_total, count, n_ref, u_ref, d_ref, t_ref, b_ref, *refs):
    o_refs, (f_s, *held_out) = refs[:count], refs[count:]
    o_ref = held_out[0] if held_out else o_refs[0]
    lat_rows = b_ref.shape[0]
    pairs = (levels + 1) // 2
    half = f_s.shape[2] // 16
    first_row = lax.axis_index("lat") * lat_rows

    def body(*accs):
        ca, da = accs[:UNITS], accs[UNITS:]
        row = lax.broadcasted_iota(jnp.int32, (SUB, 128), 0)
        lane = lax.broadcasted_iota(jnp.int32, (SUB, 128), 1)
        digits = (lax.broadcasted_iota(jnp.int32, (256, 128), 0) // SUB).astype(F32).astype(BF)
        for block in range(0, lat_rows // SUB, UNITS):
            offs, cn, cu, masks = [], [], [], []
            rows = [slice((block + q) * SUB, (block + q + 1) * SUB) for q in range(UNITS)]
            for q in range(UNITS):
                b = b_ref[rows[q], :]
                offs.append(jnp.where(b > 0, (b - 1) * HIGHS, 2 * SLOTS))
                masks.append([jnp.where(b == i + 1, 1.0, 0.0) for i in range(BASINS)])
                j = first_row + (block + q) * SUB + lax.broadcasted_iota(jnp.int32, (SUB, 128), 0)
                latitude = (-78.0 + 156.0 * (j.astype(F32) + 0.5) / lat_total) * (math.pi / 180.0)
                width = jnp.cos(latitude)
                cn.append(north_unit * width)
                cu.append(up_unit * width)

            def spot(k):
                return slice(k % half * 16, (k % half + 1) * 16), slice(k // half * 128, (k // half + 1) * 128)

            for k in range(levels, 2 * half):
                for q in range(UNITS):
                    f_s[block // UNITS, q, *spot(k)] = jnp.zeros((16, 128), BF)
            for p in range(pairs):
                lhs = [[] for _ in range(UNITS)]
                rhs = [[] for _ in range(UNITS)]
                for k in (p, p + pairs):
                    if k >= levels:
                        for q in range(UNITS):
                            lhs[q].append(jnp.zeros((2 * LOW * SUB, 128), F32))
                            rhs[q].append(jnp.zeros((256, 128), F8))
                        continue
                    both = slice(block * SUB, (block + UNITS) * SUB)
                    n16 = n_ref[0, k, both, :].astype(F32)
                    u16 = u_ref[0, k, both, :].astype(F32)
                    for q in range(UNITS):
                        part = slice(q * SUB, (q + 1) * SUB)
                        t = t_ref[k, rows[q], :]
                        north = n16[part] * cn[q] * (t.astype(F32) * 0.001)
                        rise = jnp.where(t > 0, u16[part] * cu[q], 0.0)
                        f_s[block // UNITS, q, *spot(k)] = jnp.concatenate([north, rise], 0).astype(BF)
                        d = d_ref[0, k, rows[q], :]
                        high = ((d // LOW if LOW != 8 else d >> 3) + offs[q]).astype(F32)
                        high = jnp.concatenate([high, high], 0).astype(BF)
                        low = d & (LOW - 1)
                        moving = []
                        for x in range(LOW):
                            hit = low == x
                            moving += [jnp.where(hit, north, 0.0), jnp.where(hit, rise, 0.0)]
                        lhs[q].append(jnp.concatenate(moving, 0))
                        hit = jnp.concatenate([high] * 16, 0) == digits
                        rhs[q].append(jnp.where(hit, F8(1), F8(0)))
                for q in range(UNITS):
                    pltpu.matmul_push_rhs(
                        jnp.concatenate(rhs[q], 1), staging_register=p % 2, mxu_index=q, transpose=True
                    )
                for q in range(UNITS):
                    pltpu.matmul_acc_lhs(ca[q], jnp.concatenate(lhs[q], 1), load_staged_rhs=p % 2)
            zero = jnp.zeros((SUB, 128), F32)
            for c in range(half // SUB):
                staged = (pairs + c) % 2
                for q in range(UNITS):
                    left, right = [zero] * SLOTS, [zero] * SLOTS
                    for i in range(BASINS):
                        left[i * HIGHS + c] = masks[q][i]
                        right[i * HIGHS + half // SUB + c] = masks[q][i]
                    held = jnp.concatenate([jnp.concatenate(left, 0), jnp.concatenate(right, 0)], 1)
                    pltpu.matmul_push_rhs(
                        held.astype(F8), staging_register=staged, mxu_index=q, transpose=True
                    )
                for q in range(UNITS):
                    pltpu.matmul_acc_lhs(
                        da[q], f_s[block // UNITS, q, c * 128 : (c + 1) * 128, :], load_staged_rhs=staged
                    )
            for which, acc in enumerate((ca, da)):
                for q in range(UNITS):
                    x = pltpu.matmul_pop(acc[q])
                    for s in range(2):
                        for lanes in (slice(0, 128), slice(128, 256)):
                            parts = [x[(2 * l + s) * SUB : (2 * l + s + 1) * SUB, lanes] for l in range(SUB)]
                            o_ref[which, s, rows[q], lanes] = diagonal(parts, row, lane)

    accs = [pltpu.ACC(q)((2 * LOW * SUB, 256), F32) for _ in range(2) for q in range(UNITS)]
    pl.run_scoped(body, *accs)
    if held_out:
        for m in range(count):

            @pl.when(pl.program_id(0) == m)
            def _(m=m):
                o_refs[m][...] = o_ref[...]


def lon_tables(first_month, count, lat_total, lons, each, north_vel, up_vel, dens_class, thickness, basin_id):
    _, levels, lat_rows, lon_cells = north_vel.shape
    half = -(-((levels + 1) // 2) // SUB) * SUB
    months = lons * each
    table = (2, 2, lat_rows, 256)
    vmem = pl.BlockSpec(memory_space=pltpu.VMEM)

    def month(m):
        return (lax.axis_index("lon") * each + first_month + m) % months

    def month_block():
        return pl.BlockSpec((1, levels, lat_rows, lon_cells), lambda m: (month(m), 0, 0, 0))

    blocks = lat_rows // SUB
    return pl.pallas_call(
        functools.partial(tables_kernel, levels, lat_total, count),
        grid=(count,),
        in_specs=[
            month_block(),
            month_block(),
            month_block(),
            pl.BlockSpec((levels, lat_rows, lon_cells), lambda m: (0, 0, 0)),
            pl.BlockSpec((lat_rows, lon_cells), lambda m: (0, 0)),
        ],
        out_specs=[vmem] * count,
        out_shape=[jax.ShapeDtypeStruct(table, F32)] * count,
        scratch_shapes=[pltpu.VMEM((blocks // UNITS, UNITS, half * 16, 256), BF)]
        + [pltpu.VMEM(table, F32)] * (count > 1),
        compiler_params=pltpu.CompilerParams(vmem_limit_bytes=TABLES_VMEM),
        name="tables",
    )(north_vel, up_vel, dens_class, thickness, basin_id)


def summary_kernel(*refs):
    rows = [jnp.sum(ref[w, 1], axis=0, keepdims=True) for ref in refs[:-1] for w in range(2)]
    rows.append(jnp.zeros((SUB - len(rows), 256), F32))
    refs[-1][...] = jnp.concatenate(rows, 0)


def carry_summary(tables):
    vmem = pl.BlockSpec(memory_space=pltpu.VMEM)
    return pl.pallas_call(
        summary_kernel,
        in_specs=[vmem] * len(tables),
        out_specs=vmem,
        out_shape=jax.ShapeDtypeStruct((SUB, 256), F32),
        compiler_params=pltpu.CompilerParams(vmem_limit_bytes=SMALL_VMEM),
        name="summary",
    )(*tables)


def times_binary(x, held):
    total = 0.0
    for _ in range(3):
        part = x.astype(BF)
        x = x - part.astype(F32)
        total = total + jnp.dot(part, held, preferred_element_type=F32)
    return total


def region_sums(prefix):
    row = lax.broadcasted_iota(jnp.int32, (256, 128), 0)
    column = lax.broadcasted_iota(jnp.int32, (256, 128), 1)
    basin = sum(jnp.where(row >= CLASSES * (i + 1), 1, 0) for i in range(BASINS))
    at = row - CLASSES * basin
    hit = ((at <= column) if prefix else (at == column)) & (column < CLASSES) & (basin < BASINS)
    return jnp.concatenate(
        [jnp.where(hit if r == 0 else hit & (basin == r - 1), 1.0, 0.0).astype(BF) for r in range(BASINS + 1)], 1
    )


def finish_kernel(members, levels, stream, carries, *refs):
    tables, refs = refs[:members], refs[members:]
    moved, refs = refs[:carries], refs[carries:]
    outs = refs[-4 if members == 2 else -2 :]
    kinds = len(outs) // 2
    lat_rows = tables[0].shape[2]
    row = lax.broadcasted_iota(jnp.int32, (SUB, 256), 0)
    operands = []
    for w in range(2):
        stack = []
        for e in range(members):
            x = tables[e][w, stream]
            if stream == 1:
                south = jnp.zeros((1, 256), F32)
                for s in range(1, carries + 1):
                    arrived = moved[s - 1][2 * e + w : 2 * e + w + 1, :]
                    south = south + jnp.where(lax.axis_index("lat") >= s, arrived, 0.0)
                for g in range(lat_rows // SUB):
                    y = x[g * SUB : (g + 1) * SUB]
                    for shift in (1, 2, 4):
                        y = y + jnp.where(row >= shift, pltpu.roll(y, shift, 0), 0.0)
                    y = y + south
                    south = y[SUB - 1 : SUB]
                    stack.append(y)
            else:
                stack.append(x)
        operands.append(jnp.concatenate(stack, 0))
    held = region_sums(True)
    if stream == 0:
        both = times_binary(jnp.concatenate(operands, 0), held)
        mocs = [both[: members * lat_rows], both[members * lat_rows :]]
    else:
        mocs = [times_binary(operands[0], held), times_binary(operands[1], region_sums(False))]
    for w in range(2):
        if members == 2:
            a, b = mocs[w][:lat_rows], mocs[w][lat_rows:]
            values = ((a + b) * 0.5, jnp.abs(a - b) * math.sqrt(0.5))
        else:
            values = (mocs[w],)
        size = CLASSES if w == 0 else levels
        for v, ref in zip(values, outs[:kinds] if w == 1 else outs[kinds:]):
            for r in range(BASINS + 1):
                ref[0, r, 0] = v[:, r * 128 : r * 128 + size]


def finish(tables, moved, earlier, levels, stream):
    members = len(tables)
    rows = tables[0].shape[2]
    vmem = pl.BlockSpec(memory_space=pltpu.VMEM)
    sizes = [levels] * members + [CLASSES] * members

    def out_block(size):
        return pl.BlockSpec((1, BASINS + 1, 1, rows, size), lambda m: (0, 0, stream, 0, 0))

    first = members + len(moved)
    return pl.pallas_call(
        functools.partial(finish_kernel, members, levels, stream, len(moved)),
        grid=(1,),
        in_specs=[vmem] * first + [pl.BlockSpec(memory_space=pl.ANY)] * len(earlier),
        out_specs=[out_block(size) for size in sizes],
        out_shape=[jax.ShapeDtypeStruct((1, BASINS + 1, 2, rows, size), F32) for size in sizes],
        input_output_aliases={first + i: i for i in range(len(earlier))},
        compiler_params=pltpu.CompilerParams(vmem_limit_bytes=SMALL_VMEM),
        name="finish_up" if stream else "finish_north",
    )(*tables, *moved, *earlier)


def body(north_vel, up_vel, dens_class, thickness, basin_id):
    local_members, months, levels, row_count, lon_cells = north_vel.shape
    lons, lats, mems = lax.axis_size("lon"), lax.axis_size("lat"), lax.axis_size("mem")
    each = months // lons
    members = local_members * mems

    def south(summary):
        return [lax.ppermute(summary, "lat", [(i, (i + s) % lats) for i in range(lats)]) for s in range(1, lats)]

    def one_month(tables):
        if local_members == 1 and mems == 2:
            pair = [tables[0], lax.ppermute(tables[0], "mem", [(0, 1), (1, 0)])]
            moved = south(carry_summary(pair))
            return finish(pair, moved, finish(pair, [], [], levels, 0), levels, 1)
        mocs = []
        for table in tables:
            moved = south(carry_summary([table]))
            mocs.append(finish([table], moved, finish([table], [], [], levels, 0), levels, 1))
        outs = []
        for i in range(2):
            stack = jnp.stack([moc[i] for moc in mocs])
            mean = lax.psum(jnp.sum(stack, 0), "mem") / members
            dev = lax.psum(jnp.sum(jnp.square(stack - mean), 0), "mem")
            outs += [mean, jnp.sqrt(dev / (members - 1))]
        return outs

    tables = [[] for _ in range(each)]
    for e in range(local_members):
        fields = (north_vel[e], up_vel[e], dens_class[e], thickness, basin_id)
        others = lon_tables(each, (lons - 1) * each, row_count * lats, lons, each, *fields)
        arrived = [
            [
                lax.ppermute(others[(s - 1) * each + m], "lon", [(i, (i + s) % lons) for i in range(lons)])
                for s in range(1, lons)
            ]
            for m in range(each)
        ]
        own = lon_tables(0, each, row_count * lats, lons, each, *fields)
        for m in range(each):
            tables[m].append(sum(arrived[m], own[m]))
    outs = zip(*[one_month(month) for month in tables])
    return tuple(jnp.swapaxes(jnp.concatenate(out, 0), -1, -2) for out in outs)


def solution(mesh):
    in_specs = (
        P("mem", None, None, "lat", "lon"),
        P("mem", None, None, "lat", "lon"),
        P("mem", None, None, "lat", "lon"),
        P(None, "lat", "lon"),
        P("lat", "lon"),
    )
    out_specs = (
        P("lon", None, None, None, "lat"),
        P("lon", None, None, None, "lat"),
        P("lon", None, None, None, "lat"),
        P("lon", None, None, None, "lat"),
    )
    return jax.shard_map(body, mesh=mesh, in_specs=in_specs, out_specs=out_specs, check_vma=False)
```

time: 51.1 us -> 39.1 us (0.77)
  local copies, waits for them, and re-layouts: 9.41 us -> 0 us
  Pallas kernels: 24.7 us -> 21.9 us
  waiting for transfers between devices: 4.21 us -> 4.79 us
    pallas_call x4 -> x0, local copies, waits for them, and re-layouts: 7.08 us -> none  [finish(): pl.pallas_call(functools.partial(finish_kernel, members, levels, stream,...]
    pallas_call x2, Pallas kernels: 4.46 us -> 2.07 us  [finish(): pl.pallas_call(functools.partial(finish_kernel, members, levels, stream,...]
    unnamed x10 -> x0, local copies, waits for them, and re-layouts: 1.28 us -> none
    slice x1 -> x0, local copies, waits for them, and re-layouts: 1.06 us -> none  [body(): others[(s - 1) * each:s * each]]
    ppermute x3, waiting for transfers between devices: 2.87 us -> 3.45 us  [south(): lax.ppermute(summary, 'lat', [(i, (i + s) % lats) for i in range(lats)])]
  transfers between devices with their start and end apart: 7 -> 7, of which waited for: 3 -> 3; matrix products, arithmetic and copies ran while one was open for 0% -> 0% of each run, Pallas kernels for 16% -> 18%
where the time goes in v3:
time: 39.1 us; the launch traced here: 38.9 us
  Pallas kernels  21.9 us (56%)
  starting transfers between devices  10.7 us (27%)
  waiting for transfers between devices  4.79 us (12%)
  other arithmetic  0.94 us (2%)
  between operations  0.65 us (2%)
    pallas_call x2, Pallas kernels, lon_tables(): pl.pallas_call(functools.partial(tables_kernel, levels, lat_total, count)...  19.8 us
    ppermute x3, starting transfers between devices, body(): lax.ppermute(others[(s - 1) * each + m], 'lon', [(i, (i + s) % lons) for...  5.93 us
    ppermute x3, starting transfers between devices, south(): lax.ppermute(summary, 'lat', [(i, (i + s) % lats) for i in range(lats)])  4.67 us
    ppermute x3, waiting for transfers between devices, south(): lax.ppermute(summary, 'lat', [(i, (i + s) % lats) for i in range(lats)])  3.45 us
    pallas_call x2, Pallas kernels, finish(): pl.pallas_call(functools.partial(finish_kernel, members, levels, stream,...  2.07 us
    ppermute x1, waiting for transfers between devices, one_month(): pair = [tables[0], lax.ppermute(tables[0], 'mem', [(0, 1), (1, 0)])]  1.33 us
    add x1, other arithmetic, body(): tables[m].append(sum(arrived[m], own[m]))  0.94 us
  transfers between devices with their start and end apart: 7, of which 3 were waited for; matrix products, arithmetic and copies ran while one was open for 0% of the time, Pallas kernels for 18%

profile of v3, /device:TPU:0, one launch (start us, length us, event | category | flops | bytes accessed | tf_op | source)
XLA Modules:
  0.0 38.9 jit_solution(7884473834941056102)
XLA Ops:
  0.6 13.6 %tables.3 = (f32[2,2,32,256]{3,2,1,0:T(8,128)}, f32[2,2,32,256]{3,2,1,0:T(8,128)}, f32[2,2,32,256]{3,2,1,0:T(8,128)}) custom-call(bf16[4,75,32,128]{3,2,1,0:T(8,128)(2,1)} %bitcast.9, bf16[4,75,32,128]{3,2,1,0:T(8,128)(2,1)} %bitcast.11, s32[4,75,32,128]{3,2,1,0:T(8,128)} %bitcast.7, s32[75,32,128]{2,1,0:T(8,128)} %t_ref.3, s32[32,128]{1,0:T(8,128)} %b_ref.3), custom_call_target="tpu_custom_call" | custom-call | tf_op jit(solution)/shard_map/tables/pallas_call | solution.py:160
  14.2 3.0 %collective-permute-start = (f32[2,2,32,256]{3,2,1,0:T(8,128)}, f32[2,2,32,256]{3,2,1,0:T(8,128)S(1)}, u32[]{:S(2)}, u32[]{:S(2)}) collective-permute-start(f32[2,2,32,256]{3,2,1,0:T(8,128)} %get-tuple-element.15), channel_id=1, source_target_pairs={{0,8},{8,16},{16,24},{24,0},{1,9},{9,17},{17,25},{25,1},{2,10},{10... | collective-permute-start | bytes 393224 | tf_op jit(solution)/shard_map/ppermute | solution.py:316
  17.2 1.5 %collective-permute-start.1 = (f32[2,2,32,256]{3,2,1,0:T(8,128)}, f32[2,2,32,256]{3,2,1,0:T(8,128)S(1)}, u32[]{:S(2)}, u32[]{:S(2)}) collective-permute-start(f32[2,2,32,256]{3,2,1,0:T(8,128)} %get-tuple-element.16), channel_id=1, source_target_pairs={{0,16},{8,24},{16,0},{24,8},{1,17},{9,25},{17,1},{25,9},{2,18},{10... | collective-permute-start | bytes 393224 | tf_op jit(solution)/shard_map/ppermute | solution.py:316
  18.7 1.4 %collective-permute-start.2 = (f32[2,2,32,256]{3,2,1,0:T(8,128)}, f32[2,2,32,256]{3,2,1,0:T(8,128)S(1)}, u32[]{:S(2)}, u32[]{:S(2)}) collective-permute-start(f32[2,2,32,256]{3,2,1,0:T(8,128)} %get-tuple-element.17), channel_id=1, source_target_pairs={{0,24},{8,0},{16,8},{24,16},{1,25},{9,1},{17,9},{25,17},{2,26},{10... | collective-permute-start | bytes 393224 | tf_op jit(solution)/shard_map/ppermute | solution.py:316
  20.1 6.2 %tables.2 = f32[2,2,32,256]{3,2,1,0:T(8,128)} custom-call(bf16[4,75,32,128]{3,2,1,0:T(8,128)(2,1)} %bitcast.10, bf16[4,75,32,128]{3,2,1,0:T(8,128)(2,1)} %bitcast.12, s32[4,75,32,128]{3,2,1,0:T(8,128)} %bitcast.8, s32[75,32,128]{2,1,0:T(8,128)} %t_ref.3, s32[32,128]{1,0:T(8,128)} %b_ref.3), custom_call_target="tpu_custom_call" | custom-call | tf_op jit(solution)/shard_map/tables/pallas_call | solution.py:160
  26.3 0.0 collective-permute-done
  26.3 0.0 collective-permute-done.1
  26.3 0.0 collective-permute-done.2
  26.3 0.9 %add_add_fusion.refs_0_ = f32[2,2,32,256]{3,2,1,0:T(8,128)S(1)} fusion(f32[2,2,32,256]{3,2,1,0:T(8,128)S(1)} %collective-permute-done.2, f32[2,2,32,256]{3,2,1,0:T(8,128)S(1)} %collective-permute-done.1, f32[2,2,32,256]{3,2,1,0:T(8,128)} %tables.2, f32[2,2,32,256]{3,2,1,0:T(8,128)S(1)} %collective-permute-done), kind=kLoop, calls=%fused_computation | loop fusion | flops 98304 | bytes 655360 | tf_op jit(solution)/shard_map/add | solution.py:323
  27.3 0.1 collective-permute-start.3
  27.4 1.3 %collective-permute-done.3.refs_1_ = f32[2,2,32,256]{3,2,1,0:T(8,128)S(1)} collective-permute-done((f32[2,2,32,256]{3,2,1,0:T(8,128)S(1)}, f32[2,2,32,256]{3,2,1,0:T(8,128)S(1)}, u32[]{:S(2)}, u32[]{:S(2)}) %collective-permute-start.3) | collective-permute-done | bytes 131104 | tf_op jit(solution)/shard_map/ppermute | solution.py:295
  28.7 3.7 %collective-permute-start.6 = (f32[8,256]{1,0:T(8,128)S(1)}, f32[8,256]{1,0:T(8,128)S(1)}, u32[]{:S(2)}, u32[]{:S(2)}) collective-permute-start(f32[8,256]{1,0:T(8,128)S(1)} %summary.1), channel_id=1, source_target_pairs={{0,6},{2,0},{4,2},{6,4},{1,7},{3,1},{5,3},{7,5},{8,14},{10,8},{12,... | collective-permute-start | bytes 24584 | tf_op jit(solution)/shard_map/ppermute | solution.py:291
  32.4 0.0 collective-permute-start.5
  32.4 1.0 %collective-permute-start.4 = (f32[8,256]{1,0:T(8,128)S(1)}, f32[8,256]{1,0:T(8,128)S(1)}, u32[]{:S(2)}, u32[]{:S(2)}) collective-permute-start(f32[8,256]{1,0:T(8,128)S(1)} %summary.1), channel_id=1, source_target_pairs={{0,2},{2,4},{4,6},{6,0},{1,3},{3,5},{5,7},{7,1},{8,10},{10,12},{12... | collective-permute-start | bytes 24584 | tf_op jit(solution)/shard_map/ppermute | solution.py:291
  33.4 1.0 %finish_north.1 = (f32[1,4,2,32,75]{4,3,2,1,0:T(8,128)}, f32[1,4,2,32,75]{4,3,2,1,0:T(8,128)}, f32[1,4,2,32,80]{4,3,2,1,0:T(8,128)}, f32[1,4,2,32,80]{4,3,2,1,0:T(8,128)}) custom-call(f32[2,2,32,256]{3,2,1,0:T(8,128)S(1)} %add_add_fusion.refs_0_, f32[2,2,32,256]{3,2,1,0:T(8,128)S(1)} %collective-permute-done.3.refs_1_), custom_call_target="tpu_custom_call" | custom-call | tf_op jit(solution)/shard_map/finish_north/pallas_call | solution.py:272
  34.4 0.0 collective-permute-done.6.refs_4_
  34.4 2.5 %collective-permute-done.5.refs_3_ = f32[8,256]{1,0:T(8,128)S(1)} collective-permute-done((f32[8,256]{1,0:T(8,128)S(1)}, f32[8,256]{1,0:T(8,128)S(1)}, u32[]{:S(2)}, u32[]{:S(2)}) %collective-permute-start.5) | collective-permute-done | bytes 8224 | tf_op jit(solution)/shard_map/ppermute | solution.py:291
  36.9 0.9 %collective-permute-done.4.refs_2_ = f32[8,256]{1,0:T(8,128)S(1)} collective-permute-done((f32[8,256]{1,0:T(8,128)S(1)}, f32[8,256]{1,0:T(8,128)S(1)}, u32[]{:S(2)}, u32[]{:S(2)}) %collective-permute-start.4) | collective-permute-done | bytes 8224 | tf_op jit(solution)/shard_map/ppermute | solution.py:291
  37.8 1.1 %finish_up.1 = (f32[1,4,2,32,75]{4,3,2,1,0:T(8,128)}, f32[1,4,2,32,75]{4,3,2,1,0:T(8,128)}, f32[1,4,2,32,80]{4,3,2,1,0:T(8,128)}, f32[1,4,2,32,80]{4,3,2,1,0:T(8,128)}) custom-call(f32[2,2,32,256]{3,2,1,0:T(8,128)S(1)} %add_add_fusion.refs_0_, ...), custom_call_target="tpu_custom_call", output_to_operand_aliasing={{0}: (5, {}), {1}: (6, {}), {2}: (7, {}), {3}: (8, {})} | custom-call | tf_op jit(solution)/shard_map/finish_up/pallas_call | solution.py:272
  (1 shorter events, 0.0 us)
Async XLA Ops:
  14.2 12.1 %collective-permute-start = (f32[2,2,32,256]{3,2,1,0:T(8,128)}, f32[2,2,32,256]{3,2,1,0:T(8,128)S(1)}, u32[]{:S(2)}, u32[]{:S(2)}) collective-permute-start(f32[2,2,32,256]{3,2,1,0:T(8,128)} %get-tuple-element.15), channel_id=1, source_target_pairs={{0,8},{8,16},{16,24},{24,0},{1,9},{9,17},{17,25},{25,1},{2,10},{10... | collective-permute-start | bytes 393224 | tf_op jit(solution)/shard_map/ppermute | solution.py:316
  17.2 9.2 %collective-permute-start.1 = (f32[2,2,32,256]{3,2,1,0:T(8,128)}, f32[2,2,32,256]{3,2,1,0:T(8,128)S(1)}, u32[]{:S(2)}, u32[]{:S(2)}) collective-permute-start(f32[2,2,32,256]{3,2,1,0:T(8,128)} %get-tuple-element.16), channel_id=1, source_target_pairs={{0,16},{8,24},{16,0},{24,8},{1,17},{9,25},{17,1},{25,9},{2,18},{10... | collective-permute-start | bytes 393224 | tf_op jit(solution)/shard_map/ppermute | solution.py:316
  18.7 7.6 %collective-permute-start.2 = (f32[2,2,32,256]{3,2,1,0:T(8,128)}, f32[2,2,32,256]{3,2,1,0:T(8,128)S(1)}, u32[]{:S(2)}, u32[]{:S(2)}) collective-permute-start(f32[2,2,32,256]{3,2,1,0:T(8,128)} %get-tuple-element.17), channel_id=1, source_target_pairs={{0,24},{8,0},{16,8},{24,16},{1,25},{9,1},{17,9},{25,17},{2,26},{10... | collective-permute-start | bytes 393224 | tf_op jit(solution)/shard_map/ppermute | solution.py:316
  27.3 1.4 %collective-permute-start.3 = (f32[2,2,32,256]{3,2,1,0:T(8,128)S(1)}, f32[2,2,32,256]{3,2,1,0:T(8,128)S(1)}, u32[]{:S(2)}, u32[]{:S(2)}) collective-permute-start(f32[2,2,32,256]{3,2,1,0:T(8,128)S(1)} %add_add_fusion.refs_0_), channel_id=1, source_target_pairs={{0,1},{1,0},{2,3},{3,2},{4,5},{5,4},{6,7},{7,6},{8,9},{9,8},{10,11... | collective-permute-start | bytes 393224 | tf_op jit(solution)/shard_map/ppermute | solution.py:295
  28.7 5.7 %collective-permute-start.6 = (f32[8,256]{1,0:T(8,128)S(1)}, f32[8,256]{1,0:T(8,128)S(1)}, u32[]{:S(2)}, u32[]{:S(2)}) collective-permute-start(f32[8,256]{1,0:T(8,128)S(1)} %summary.1), channel_id=1, source_target_pairs={{0,6},{2,0},{4,2},{6,4},{1,7},{3,1},{5,3},{7,5},{8,14},{10,8},{12,... | collective-permute-start | bytes 24584 | tf_op jit(solution)/shard_map/ppermute | solution.py:291
  32.4 4.5 %collective-permute-start.5 = (f32[8,256]{1,0:T(8,128)S(1)}, f32[8,256]{1,0:T(8,128)S(1)}, u32[]{:S(2)}, u32[]{:S(2)}) collective-permute-start(f32[8,256]{1,0:T(8,128)S(1)} %summary.1), channel_id=1, source_target_pairs={{0,4},{2,6},{4,0},{6,2},{1,5},{3,7},{5,1},{7,3},{8,12},{10,14},{12... | collective-permute-start | bytes 24584 | tf_op jit(solution)/shard_map/ppermute | solution.py:291
  32.4 5.4 %collective-permute-start.4 = (f32[8,256]{1,0:T(8,128)S(1)}, f32[8,256]{1,0:T(8,128)S(1)}, u32[]{:S(2)}, u32[]{:S(2)}) collective-permute-start(f32[8,256]{1,0:T(8,128)S(1)} %summary.1), channel_id=1, source_target_pairs={{0,2},{2,4},{4,6},{6,0},{1,3},{3,5},{5,7},{7,1},{8,10},{10,12},{12... | collective-permute-start | bytes 24584 | tf_op jit(solution)/shard_map/ppermute | solution.py:291

commit v4 on v3

--- a/solution.py
+++ b/solution.py
@@ -16,7 +16,7 @@
 SLOTS = 256 // SUB
 UNITS = 2
 
-TABLES_VMEM = 60 << 20
+TABLES_VMEM = 24 << 20
 SMALL_VMEM = 8 << 20
 
 north_unit = 0.02
@@ -42,10 +42,70 @@
     return parts[0]
 
 
-def tables_kernel(levels, lat_total, count, n_ref, u_ref, d_ref, t_ref, b_ref, *refs):
-    o_refs, (f_s, *held_out) = refs[:count], refs[count:]
-    o_ref = held_out[0] if held_out else o_refs[0]
-    lat_rows = b_ref.shape[0]
+def fetches(levels, lat_rows, months, hbm, vmem, sem):
+    pairs = (levels + 1) // 2
+    tall = UNITS * SUB
+    plan, used = [], 0
+
+    def copy(src, dst):
+        nonlocal used
+        used += 1
+        return pltpu.make_async_copy(src, dst, sem.at[used - 1])
+
+    *hbm, b = hbm
+    *vmem, b_s = vmem
+    for m, month in enumerate(months):
+        for gp in range(lat_rows // tall):
+            rows = pl.ds(gp * tall, tall)
+            start = m == 0 and gp == 0
+            cuts = [0, pairs // 5, pairs // 2, pairs] if start else [0, pairs]
+            parts = []
+            for first, last in zip(cuts, cuts[1:]):
+                copies = [copy(b, b_s)] if used == 0 else []
+                spans = [(first, last), (first + pairs, min(last + pairs, levels))] if start else [(0, levels)]
+                for k0, k1 in spans:
+                    span = pl.ds(k0, k1 - k0)
+                    for i, (src, dst) in enumerate(zip(hbm, vmem)):
+                        if i < 3:
+                            src, dst = src.at[month], dst.at[m]
+                        elif m > 0:
+                            continue
+                        copies.append(copy(src.at[span, rows, :], dst.at[span, rows, :]))
+                parts.append((first, copies))
+            plan.append(parts)
+    return plan
+
+
+def copy_count(count, blocks):
+    pairs = blocks // UNITS
+    return 1 + 3 * 2 * 4 + (pairs - 1) * 4 + (count - 1) * pairs * 3
+
+
+def tables_kernel(levels, lat_total, count, month, rest, *refs):
+    fields, refs = refs[:5], refs[5:]
+    o_refs, refs = refs[:count], refs[count:]
+    lat_rows = fields[4].shape[0]
+    plan, kept = [], []
+    if month is None:
+        (f_s,) = refs
+        local = fields
+    else:
+        keep, refs = refs[: 3 * len(rest)], refs[3 * len(rest) :]
+        t_keep, b_keep, f_s, *scratch, sem, keep_sem = refs
+        local = [*scratch, t_keep, b_keep]
+        plan = fetches(levels, lat_rows, [month(m) for m in range(count)], fields, local, sem)
+        for parts in plan:
+            for _, copies in parts:
+                for c in copies:
+                    c.start()
+        for i, months in enumerate(rest):
+            for f in range(3):
+                for m in range(len(months)):
+                    at = keep_sem.at[len(kept)]
+                    kept.append(pltpu.make_async_copy(fields[f].at[month(months[m])], keep[3 * i + f].at[m], at))
+        for c in kept:
+            c.start()
+    n_ref, u_ref, d_ref, t_ref, b_ref = local
     pairs = (levels + 1) // 2
     half = f_s.shape[2] // 16
     first_row = lax.axis_index("lat") * lat_rows
@@ -55,7 +115,16 @@
         row = lax.broadcasted_iota(jnp.int32, (SUB, 128), 0)
         lane = lax.broadcasted_iota(jnp.int32, (SUB, 128), 1)
         digits = (lax.broadcasted_iota(jnp.int32, (256, 128), 0) // SUB).astype(F32).astype(BF)
-        for block in range(0, lat_rows // SUB, UNITS):
+        for m, block in [(m, block) for m in range(count) for block in range(0, lat_rows // SUB, UNITS)]:
+            unit = m * (lat_rows // SUB // UNITS) + block // UNITS
+            waits = dict(plan[0]) if unit == 0 and plan else {}
+            if unit + 1 < len(plan):
+                waits[pairs - 8] = [c for _, copies in plan[unit + 1] for c in copies]
+            elif plan:
+                waits[pairs - 8] = kept
+            for c in waits.pop(0, []):
+                c.wait()
+            o_ref = o_refs[m]
             offs, cn, cu, masks = [], [], [], []
             rows = [slice((block + q) * SUB, (block + q + 1) * SUB) for q in range(UNITS)]
             for q in range(UNITS):
@@ -75,6 +144,8 @@
                 for q in range(UNITS):
                     f_s[block // UNITS, q, *spot(k)] = jnp.zeros((16, 128), BF)
             for p in range(pairs):
+                for c in waits.pop(p, []):
+                    c.wait()
                 lhs = [[] for _ in range(UNITS)]
                 rhs = [[] for _ in range(UNITS)]
                 for k in (p, p + pairs):
@@ -84,15 +155,15 @@
                             rhs[q].append(jnp.zeros((256, 128), F8))
                         continue
                     both = slice(block * SUB, (block + UNITS) * SUB)
-                    n16 = n_ref[0, k, both, :].astype(F32)
-                    u16 = u_ref[0, k, both, :].astype(F32)
+                    n16 = n_ref[m, k, both, :].astype(F32)
+                    u16 = u_ref[m, k, both, :].astype(F32)
                     for q in range(UNITS):
                         part = slice(q * SUB, (q + 1) * SUB)
                         t = t_ref[k, rows[q], :]
                         north = n16[part] * cn[q] * (t.astype(F32) * 0.001)
                         rise = jnp.where(t > 0, u16[part] * cu[q], 0.0)
                         f_s[block // UNITS, q, *spot(k)] = jnp.concatenate([north, rise], 0).astype(BF)
-                        d = d_ref[0, k, rows[q], :]
+                        d = d_ref[m, k, rows[q], :]
                         high = ((d // LOW if LOW != 8 else d >> 3) + offs[q]).astype(F32)
                         high = jnp.concatenate([high, high], 0).astype(BF)
                         low = d & (LOW - 1)
@@ -135,45 +206,33 @@
 
     accs = [pltpu.ACC(q)((2 * LOW * SUB, 256), F32) for _ in range(2) for q in range(UNITS)]
     pl.run_scoped(body, *accs)
-    if held_out:
-        for m in range(count):
-
-            @pl.when(pl.program_id(0) == m)
-            def _(m=m):
-                o_refs[m][...] = o_ref[...]
-
-
-def lon_tables(first_month, count, lat_total, lons, each, north_vel, up_vel, dens_class, thickness, basin_id):
-    _, levels, lat_rows, lon_cells = north_vel.shape
+
+
+def lon_tables(count, lat_total, month, rest, fields):
+    levels, lat_rows, lon_cells = fields[3].shape
     half = -(-((levels + 1) // 2) // SUB) * SUB
-    months = lons * each
-    table = (2, 2, lat_rows, 256)
+    blocks = lat_rows // SUB
     vmem = pl.BlockSpec(memory_space=pltpu.VMEM)
-
-    def month(m):
-        return (lax.axis_index("lon") * each + first_month + m) % months
-
-    def month_block():
-        return pl.BlockSpec((1, levels, lat_rows, lon_cells), lambda m: (month(m), 0, 0, 0))
-
-    blocks = lat_rows // SUB
+    outs = [jax.ShapeDtypeStruct((2, 2, lat_rows, 256), F32)] * count
+    scratch = [pltpu.VMEM((blocks // UNITS, UNITS, half * 16, 256), BF)]
+    if month is not None:
+        fields = [pltpu.with_memory_space_constraint(x, pltpu.HBM) for x in fields]
+        outs = outs + [jax.ShapeDtypeStruct((len(ms), *x.shape[1:]), x.dtype) for ms in rest for x in fields[:3]]
+        outs = outs + [jax.ShapeDtypeStruct(x.shape, x.dtype) for x in fields[3:]]
+        scratch += [pltpu.VMEM((count, *x.shape[1:]), x.dtype) for x in fields[:3]]
+        scratch += [
+            pltpu.SemaphoreType.DMA((copy_count(count, blocks),)),
+            pltpu.SemaphoreType.DMA((3 * sum(len(ms) for ms in rest),)),
+        ]
     return pl.pallas_call(
-        functools.partial(tables_kernel, levels, lat_total, count),
-        grid=(count,),
-        in_specs=[
-            month_block(),
-            month_block(),
-            month_block(),
-            pl.BlockSpec((levels, lat_rows, lon_cells), lambda m: (0, 0, 0)),
-            pl.BlockSpec((lat_rows, lon_cells), lambda m: (0, 0)),
-        ],
-        out_specs=[vmem] * count,
-        out_shape=[jax.ShapeDtypeStruct(table, F32)] * count,
-        scratch_shapes=[pltpu.VMEM((blocks // UNITS, UNITS, half * 16, 256), BF)]
-        + [pltpu.VMEM(table, F32)] * (count > 1),
+        functools.partial(tables_kernel, levels, lat_total, count, month, rest),
+        in_specs=[vmem if month is None else pl.BlockSpec(memory_space=pltpu.HBM)] * 5,
+        out_specs=[vmem] * len(outs),
+        out_shape=outs,
+        scratch_shapes=scratch,
         compiler_params=pltpu.CompilerParams(vmem_limit_bytes=TABLES_VMEM),
         name="tables",
-    )(north_vel, up_vel, dens_class, thickness, basin_id)
+    )(*fields)
 
 
 def summary_kernel(*refs):
@@ -307,20 +366,46 @@
             outs += [mean, jnp.sqrt(dev / (members - 1))]
         return outs
 
+    if lons & (lons - 1) == 0:
+        hops = list(range(lons - 1, -1, -1))
+
+        def owner(i, hop):
+            return i ^ hop
+    else:
+        hops = list(range(1, lons + 1))
+
+        def owner(i, hop):
+            return (i + hop) % lons
+
+    todo = [(hop, m) for hop in hops for m in range(each)]
+    calls = [call for call in (todo[:-each], todo[-each:]) if call]
+
+    def month(item):
+        hop, m = item
+        if hop == 0 or hop == lons:
+            return lax.axis_index("lon") * each + m
+        mine = lax.axis_index("lon")
+        target = mine ^ hop if lons & (lons - 1) == 0 else lax.rem(mine + hop, lons)
+        return target * each + m
+
     tables = [[] for _ in range(each)]
     for e in range(local_members):
         fields = (north_vel[e], up_vel[e], dens_class[e], thickness, basin_id)
-        others = lon_tables(each, (lons - 1) * each, row_count * lats, lons, each, *fields)
-        arrived = [
-            [
-                lax.ppermute(others[(s - 1) * each + m], "lon", [(i, (i + s) % lons) for i in range(lons)])
-                for s in range(1, lons)
-            ]
-            for m in range(each)
-        ]
-        own = lon_tables(0, each, row_count * lats, lons, each, *fields)
+        parts = [[] for _ in range(each)]
+        for i, call in enumerate(calls):
+            if i == 0:
+                at = lambda x: month(call[x] if isinstance(x, int) else x)
+                made = lon_tables(len(call), row_count * lats, at, calls[1:], fields)
+                kept = made[len(call) :]
+            else:
+                at = 3 * (i - 1)
+                made = lon_tables(len(call), row_count * lats, None, [], (*kept[at : at + 3], *kept[-2:]))
+            for (hop, m), table in zip(call, made):
+                if hop % lons:
+                    table = lax.ppermute(table, "lon", [(j, owner(j, hop)) for j in range(lons)])
+                parts[m].append(table)
         for m in range(each):
-            tables[m].append(sum(arrived[m], own[m]))
+            tables[m].append(sum(parts[m][1:], parts[m][0]))
     outs = zip(*[one_month(month) for month in tables])
     return tuple(jnp.swapaxes(jnp.concatenate(out, 0), -1, -2) for out in outs)
 

time: 39.1 us -> 34.9 us (0.89)
  Pallas kernels: 21.9 us -> 17.6 us
  waiting for transfers between devices: 4.79 us -> 6.99 us
  starting transfers between devices: 10.7 us -> 9.37 us
  other arithmetic: 0.94 us -> 0.03 us
    pallas_call x2, Pallas kernels: 19.8 us -> 15.5 us  [lon_tables(): pl.pallas_call(functools.partial(tables_kernel, levels, lat_total, count,...]
    ppermute x3, waiting for transfers between devices: 0.01 us -> 2.2 us  [body(): lax.ppermute(table, 'lon', [(j, owner(j, hop)) for j in range(lons)])]
    ppermute x3, starting transfers between devices: 5.93 us -> 4.63 us  [body(): lax.ppermute(table, 'lon', [(j, owner(j, hop)) for j in range(lons)])]
    add x1, other arithmetic: 0.94 us -> 0.03 us  [body(): tables[m].append(sum(parts[m][1:], parts[m][0]))]
  transfers between devices with their start and end apart: 7 -> 7, of which waited for: 3 -> 5; matrix products, arithmetic and copies ran while one was open for 0% -> 0% of each run, Pallas kernels for 18% -> 13%
where the time goes in v4:
time: 34.9 us; the launch traced here: 34.6 us
  Pallas kernels  17.6 us (50%)
  starting transfers between devices  9.37 us (27%)
  waiting for transfers between devices  6.99 us (20%)
  between operations  0.68 us (2%)
    pallas_call x2, Pallas kernels, lon_tables(): pl.pallas_call(functools.partial(tables_kernel, levels, lat_total, count,...  15.5 us
    ppermute x3, starting transfers between devices, south(): lax.ppermute(summary, 'lat', [(i, (i + s) % lats) for i in range(lats)])  4.67 us
    ppermute x3, starting transfers between devices, body(): lax.ppermute(table, 'lon', [(j, owner(j, hop)) for j in range(lons)])  4.63 us
    ppermute x3, waiting for transfers between devices, south(): lax.ppermute(summary, 'lat', [(i, (i + s) % lats) for i in range(lats)])  3.46 us
    ppermute x3, waiting for transfers between devices, body(): lax.ppermute(table, 'lon', [(j, owner(j, hop)) for j in range(lons)])  2.2 us
    pallas_call x2, Pallas kernels, finish(): pl.pallas_call(functools.partial(finish_kernel, members, levels, stream,...  2.07 us
    ppermute x1, waiting for transfers between devices, one_month(): pair = [tables[0], lax.ppermute(tables[0], 'mem', [(0, 1), (1, 0)])]  1.33 us
  transfers between devices with their start and end apart: 7, of which 5 were waited for; matrix products, arithmetic and copies ran while one was open for 0% of the time, Pallas kernels for 13%

profile of v4, /device:TPU:0, one launch (start us, length us, event | category | flops | bytes accessed | tf_op | source)
XLA Modules:
  0.0 34.6 jit_solution(17087393603899476700)
XLA Ops:
  0.6 11.8 %tables.2 = (f32[2,2,32,256]{3,2,1,0:T(8,128)S(1)}, f32[2,2,32,256]{3,2,1,0:T(8,128)S(1)}, f32[2,2,32,256]{3,2,1,0:T(8,128)S(1)}, bf16[1,75,32,128]{3,2,1,0:T(8,...) custom-call(bf16[4,75,32,128]{3,2,1,0:T(8,128)(2,1)} %bitcast.8, ...), custom_call_target="tpu_custom_call" | custom-call | tf_op jit(solution)/shard_map/tables/pallas_call | solution.py:227
  12.4 4.0 %collective-permute-start = (f32[2,2,32,256]{3,2,1,0:T(8,128)S(1)}, f32[2,2,32,256]{3,2,1,0:T(8,128)S(1)}, u32[]{:S(2)}, u32[]{:S(2)}) collective-permute-start(f32[2,2,32,256]{3,2,1,0:T(8,128)S(1)} %get-tuple-element.20), channel_id=1, source_target_pairs={{0,24},{8,16},{16,8},{24,0},{1,25},{9,17},{17,9},{25,1},{2,26},{10... | collective-permute-start | bytes 393224 | tf_op jit(solution)/shard_map/ppermute | solution.py:405
  16.4 0.5 %collective-permute-start.1 = (f32[2,2,32,256]{3,2,1,0:T(8,128)S(1)}, f32[2,2,32,256]{3,2,1,0:T(8,128)S(1)}, u32[]{:S(2)}, u32[]{:S(2)}) collective-permute-start(f32[2,2,32,256]{3,2,1,0:T(8,128)S(1)} %get-tuple-element.21), channel_id=1, source_target_pairs={{0,16},{8,24},{16,0},{24,8},{1,17},{9,25},{17,1},{25,9},{2,18},{10... | collective-permute-start | bytes 393224 | tf_op jit(solution)/shard_map/ppermute | solution.py:405
  16.9 0.1 collective-permute-start.2
  17.1 3.7 %tables.3 = f32[2,2,32,256]{3,2,1,0:T(8,128)S(1)} custom-call(bf16[1,75,32,128]{3,2,1,0:T(8,128)(2,1)S(1)} %get-tuple-element.23.refs_0_, bf16[1,75,32,128]{3,2,1,0:T(8,128)(2,1)S(1)} %get-tuple-element.24.refs_1_, s32[1,75,32,128]{3,2,1,0:T(8,128)S(1)} %get-tuple-element.25.refs_2_, s32[75,32,128]{2,1,0:T(8,128)S(1)} %get-tuple-element.26.refs_3_, ...), custom_call_target="tpu_custom_call" | custom-call | tf_op jit(solution)/shard_map/tables/pallas_call | solution.py:227
  20.8 0.0 collective-permute-done
  20.8 1.9 %collective-permute-done.1 = f32[2,2,32,256]{3,2,1,0:T(8,128)S(1)} collective-permute-done((f32[2,2,32,256]{3,2,1,0:T(8,128)S(1)}, f32[2,2,32,256]{3,2,1,0:T(8,128)S(1)}, u32[]{:S(2)}, u32[]{:S(2)}) %collective-permute-start.1) | collective-permute-done | bytes 131104 | tf_op jit(solution)/shard_map/ppermute | solution.py:405
  22.7 0.3 collective-permute-done.2
  23.0 0.1 collective-permute-start.3
  23.1 1.3 %collective-permute-done.3.refs_1_ = f32[2,2,32,256]{3,2,1,0:T(8,128)S(1)} collective-permute-done((f32[2,2,32,256]{3,2,1,0:T(8,128)S(1)}, f32[2,2,32,256]{3,2,1,0:T(8,128)S(1)}, u32[]{:S(2)}, u32[]{:S(2)}) %collective-permute-start.3) | collective-permute-done | bytes 131104 | tf_op jit(solution)/shard_map/ppermute | solution.py:354
  24.4 3.7 %collective-permute-start.6 = (f32[8,256]{1,0:T(8,128)S(1)}, f32[8,256]{1,0:T(8,128)S(1)}, u32[]{:S(2)}, u32[]{:S(2)}) collective-permute-start(f32[8,256]{1,0:T(8,128)S(1)} %summary.1), channel_id=1, source_target_pairs={{0,6},{2,0},{4,2},{6,4},{1,7},{3,1},{5,3},{7,5},{8,14},{10,8},{12,... | collective-permute-start | bytes 24584 | tf_op jit(solution)/shard_map/ppermute | solution.py:350
  28.1 0.0 collective-permute-start.5
  28.1 1.0 %collective-permute-start.4 = (f32[8,256]{1,0:T(8,128)S(1)}, f32[8,256]{1,0:T(8,128)S(1)}, u32[]{:S(2)}, u32[]{:S(2)}) collective-permute-start(f32[8,256]{1,0:T(8,128)S(1)} %summary.1), channel_id=1, source_target_pairs={{0,2},{2,4},{4,6},{6,0},{1,3},{3,5},{5,7},{7,1},{8,10},{10,12},{12... | collective-permute-start | bytes 24584 | tf_op jit(solution)/shard_map/ppermute | solution.py:350
  29.1 1.0 %finish_north.1 = (f32[1,4,2,32,75]{4,3,2,1,0:T(8,128)}, f32[1,4,2,32,75]{4,3,2,1,0:T(8,128)}, f32[1,4,2,32,80]{4,3,2,1,0:T(8,128)}, f32[1,4,2,32,80]{4,3,2,1,0:T(8,128)}) custom-call(f32[2,2,32,256]{3,2,1,0:T(8,128)S(1)} %add_add_fusion.refs_0_, f32[2,2,32,256]{3,2,1,0:T(8,128)S(1)} %collective-permute-done.3.refs_1_), custom_call_target="tpu_custom_call" | custom-call | tf_op jit(solution)/shard_map/finish_north/pallas_call | solution.py:331
  30.1 0.0 collective-permute-done.6.refs_4_
  30.1 2.6 %collective-permute-done.5.refs_3_ = f32[8,256]{1,0:T(8,128)S(1)} collective-permute-done((f32[8,256]{1,0:T(8,128)S(1)}, f32[8,256]{1,0:T(8,128)S(1)}, u32[]{:S(2)}, u32[]{:S(2)}) %collective-permute-start.5) | collective-permute-done | bytes 8224 | tf_op jit(solution)/shard_map/ppermute | solution.py:350
  32.6 0.9 %collective-permute-done.4.refs_2_ = f32[8,256]{1,0:T(8,128)S(1)} collective-permute-done((f32[8,256]{1,0:T(8,128)S(1)}, f32[8,256]{1,0:T(8,128)S(1)}, u32[]{:S(2)}, u32[]{:S(2)}) %collective-permute-start.4) | collective-permute-done | bytes 8224 | tf_op jit(solution)/shard_map/ppermute | solution.py:350
  33.5 1.1 %finish_up.1 = (f32[1,4,2,32,75]{4,3,2,1,0:T(8,128)}, f32[1,4,2,32,75]{4,3,2,1,0:T(8,128)}, f32[1,4,2,32,80]{4,3,2,1,0:T(8,128)}, f32[1,4,2,32,80]{4,3,2,1,0:T(8,128)}) custom-call(f32[2,2,32,256]{3,2,1,0:T(8,128)S(1)} %add_add_fusion.refs_0_, ...), custom_call_target="tpu_custom_call", output_to_operand_aliasing={{0}: (5, {}), {1}: (6, {}), {2}: (7, {}), {3}: (8, {})} | custom-call | tf_op jit(solution)/shard_map/finish_up/pallas_call | solution.py:331
  (2 shorter events, 0.1 us)
Async XLA Ops:
  12.4 8.3 %collective-permute-start = (f32[2,2,32,256]{3,2,1,0:T(8,128)S(1)}, f32[2,2,32,256]{3,2,1,0:T(8,128)S(1)}, u32[]{:S(2)}, u32[]{:S(2)}) collective-permute-start(f32[2,2,32,256]{3,2,1,0:T(8,128)S(1)} %get-tuple-element.20), channel_id=1, source_target_pairs={{0,24},{8,16},{16,8},{24,0},{1,25},{9,17},{17,9},{25,1},{2,26},{10... | collective-permute-start | bytes 393224 | tf_op jit(solution)/shard_map/ppermute | solution.py:405
  16.4 6.3 %collective-permute-start.1 = (f32[2,2,32,256]{3,2,1,0:T(8,128)S(1)}, f32[2,2,32,256]{3,2,1,0:T(8,128)S(1)}, u32[]{:S(2)}, u32[]{:S(2)}) collective-permute-start(f32[2,2,32,256]{3,2,1,0:T(8,128)S(1)} %get-tuple-element.21), channel_id=1, source_target_pairs={{0,16},{8,24},{16,0},{24,8},{1,17},{9,25},{17,1},{25,9},{2,18},{10... | collective-permute-start | bytes 393224 | tf_op jit(solution)/shard_map/ppermute | solution.py:405
  16.9 6.0 %collective-permute-start.2 = (f32[2,2,32,256]{3,2,1,0:T(8,128)S(1)}, f32[2,2,32,256]{3,2,1,0:T(8,128)S(1)}, u32[]{:S(2)}, u32[]{:S(2)}) collective-permute-start(f32[2,2,32,256]{3,2,1,0:T(8,128)S(1)} %get-tuple-element.22), channel_id=1, source_target_pairs={{0,8},{8,0},{16,24},{24,16},{1,9},{9,1},{17,25},{25,17},{2,10},{10... | collective-permute-start | bytes 393224 | tf_op jit(solution)/shard_map/ppermute | solution.py:405
  23.0 1.4 %collective-permute-start.3 = (f32[2,2,32,256]{3,2,1,0:T(8,128)S(1)}, f32[2,2,32,256]{3,2,1,0:T(8,128)S(1)}, u32[]{:S(2)}, u32[]{:S(2)}) collective-permute-start(f32[2,2,32,256]{3,2,1,0:T(8,128)S(1)} %add_add_fusion.refs_0_), channel_id=1, source_target_pairs={{0,1},{1,0},{2,3},{3,2},{4,5},{5,4},{6,7},{7,6},{8,9},{9,8},{10,11... | collective-permute-start | bytes 393224 | tf_op jit(solution)/shard_map/ppermute | solution.py:354
  24.4 5.7 %collective-permute-start.6 = (f32[8,256]{1,0:T(8,128)S(1)}, f32[8,256]{1,0:T(8,128)S(1)}, u32[]{:S(2)}, u32[]{:S(2)}) collective-permute-start(f32[8,256]{1,0:T(8,128)S(1)} %summary.1), channel_id=1, source_target_pairs={{0,6},{2,0},{4,2},{6,4},{1,7},{3,1},{5,3},{7,5},{8,14},{10,8},{12,... | collective-permute-start | bytes 24584 | tf_op jit(solution)/shard_map/ppermute | solution.py:350
  28.1 4.5 %collective-permute-start.5 = (f32[8,256]{1,0:T(8,128)S(1)}, f32[8,256]{1,0:T(8,128)S(1)}, u32[]{:S(2)}, u32[]{:S(2)}) collective-permute-start(f32[8,256]{1,0:T(8,128)S(1)} %summary.1), channel_id=1, source_target_pairs={{0,4},{2,6},{4,0},{6,2},{1,5},{3,7},{5,1},{7,3},{8,12},{10,14},{12... | collective-permute-start | bytes 24584 | tf_op jit(solution)/shard_map/ppermute | solution.py:350
  28.1 5.4 %collective-permute-start.4 = (f32[8,256]{1,0:T(8,128)S(1)}, f32[8,256]{1,0:T(8,128)S(1)}, u32[]{:S(2)}, u32[]{:S(2)}) collective-permute-start(f32[8,256]{1,0:T(8,128)S(1)} %summary.1), channel_id=1, source_target_pairs={{0,2},{2,4},{4,6},{6,0},{1,3},{3,5},{5,7},{7,1},{8,10},{10,12},{12... | collective-permute-start | bytes 24584 | tf_op jit(solution)/shard_map/ppermute | solution.py:350
